TPU v7x, 256 devices: a whole 4x4x8 slice. The times are simulated.
256 devices in a mesh: dp: 16 (over z, y_lo), mp: 16 (over y_hi, x, core).
Axes of the slice: x: 4, y: 4 (y_hi: 2, y_lo: 2; y = y_hi * 2 + y_lo), z: 8, core: 2. Of those that a mesh axis runs over, the one named last changes fastest.
Arguments:
- gradient: bfloat16 [1, 4096, 4096], P(None, 'mp', 'dp'), may hold values from -6 to 6
- first_moment: float32 [1, 4096, 4096], P(None, 'mp', 'dp'), may hold values from -3 to 3
- second_moment: float32 [1, 4096, 4096], P(None, 'mp', 'dp'), may hold values from 0.0625 to 1
- left_factor: float32 [1, 4096, 4096], P(None, 'mp', 'dp'), may hold values from -18 to 18
- right_factor: float32 [1, 4096, 4096], P(None, 'mp', 'dp'), may hold values from -18 to 18
- left_basis: bfloat16 [1, 4096, 4096], P(None, 'dp', 'mp'), may hold values from -0.09375 to 0.09375
- right_basis: bfloat16 [1, 4096, 4096], P(None, 'mp', 'dp'), may hold values from -0.09375 to 0.09375
Outputs:
- new_first_moment: float32 [1, 4096, 4096], P(None, 'mp', 'dp')
- new_second_moment: float32 [1, 4096, 4096], P(None, 'mp', 'dp')
- new_left_factor: float32 [1, 4096, 4096], P(None, 'mp', 'dp')
- new_right_factor: float32 [1, 4096, 4096], P(None, 'mp', 'dp')
- update: bfloat16 [1, 4096, 4096], P(None, 'mp', 'dp')
All inputs are finite; a program needn't handle non-finite values.
Results may differ from a plain program's by a relative error of at most 0.014.
Values may be sent and summed in bfloat16 or wider, within the bound.
A program may use at most 64 MiB of HBM per device.

v0:
```python
import jax
import jax.numpy as jnp
from jax import lax
from jax.sharding import PartitionSpec as P

decay_moment = 0.95
decay_factor = 0.95
epsilon = 1e-08


def in_one_piece(arrays, axis, dim, along):
    widths = [a.shape[along] for a in arrays]
    both = jnp.concatenate(arrays, axis=along)
    whole = lax.all_gather(both, axis, axis=dim, tiled=True)
    return tuple(jnp.split(whole, [sum(widths[:k]) for k in range(1, len(widths))], axis=along))


def turned_gather(arrays, axis, dims):
    turned = [jnp.moveaxis(a, dim, 0) for a, dim in zip(arrays, dims)]
    both = jnp.concatenate([t.reshape(len(t), -1) for t in turned], axis=1)
    whole, at, gathered = (lax.all_gather(both, axis, axis=0, tiled=True), 0, [])
    for t, dim in zip(turned, dims):
        section = whole[:, at : at + t[0].size].reshape(-1, *t.shape[1:])
        gathered.append(jnp.moveaxis(section, 0, dim))
        at += t[0].size
    return tuple(gathered)


def in_order(pieces, dim):
    lengths = list(pieces.shape[1:])
    lengths[dim] *= pieces.shape[0]
    return jnp.moveaxis(pieces, 0, dim).reshape(lengths)


def from_everyone(x, axis):
    length = lax.axis_size(axis)
    return lax.all_to_all(jnp.broadcast_to(x[None], (length, *x.shape)), axis, 0, 0, tiled=True)


def collect(x, axis, dim):
    return in_order(from_everyone(x, axis), dim)


def split_up(x, dim, length):
    lengths = x.shape
    pieces = x.reshape(*lengths[:dim], length, lengths[dim] // length, *lengths[dim + 1 :])
    return jnp.moveaxis(pieces, dim, 0)


def summed_on_arrival(x, axis, dim):
    pieces = split_up(x, dim, lax.axis_size(axis))
    arrived = lax.all_to_all(pieces, axis, split_axis=0, concat_axis=0, tiled=True)
    return arrived.astype(jnp.float32).sum(axis=0)


def per_device(
    gradient, first_moment, second_moment, left_factor, right_factor, left_basis, right_basis
):
    scale = 1.0 - decay_factor
    column_grad, column_right = in_one_piece((gradient, right_basis), "mp", 1, 0)
    row_grad, column_left = turned_gather((gradient, left_basis), "dp", (2, 1))
    row_block = lax.all_to_all(column_grad, "dp", split_axis=1, concat_axis=2, tiled=True)
    column_block = lax.all_to_all(row_grad, "mp", split_axis=2, concat_axis=1, tiled=True)
    left_sum = jnp.einsum("brc,bkc->brk", row_grad, row_block, preferred_element_type=jnp.float32)
    right_sum = jnp.einsum(
        "bkr,bkc->brc", column_block, column_grad, preferred_element_type=jnp.float32
    )
    rotated_left = jnp.einsum(
        "bkr,bkc->brc", column_left, column_grad, preferred_element_type=jnp.float32
    ).astype(jnp.bfloat16)
    rotated = jnp.einsum(
        "brn,bnc->brc",
        collect(rotated_left, "dp", 2),
        column_right,
        preferred_element_type=jnp.float32,
    )
    new_first = decay_moment * first_moment + (1.0 - decay_moment) * rotated
    new_second = decay_moment * second_moment + (1.0 - decay_moment) * rotated * rotated
    direction = (new_first / (jnp.sqrt(new_second) + epsilon)).astype(jnp.bfloat16)
    back_term = jnp.einsum(
        "bkr,brc->bkc", column_left, direction, preferred_element_type=jnp.float32
    )
    back_sum = summed_on_arrival(back_term.astype(jnp.bfloat16), "mp", 1)
    back_rows = back_sum.astype(jnp.bfloat16)
    update_term = jnp.einsum(
        "brc,bkc->brk", back_rows, column_right, preferred_element_type=jnp.float32
    )
    update_sum = summed_on_arrival(update_term.astype(jnp.bfloat16), "dp", 2)
    new_left = decay_factor * left_factor + scale * left_sum
    new_right = decay_factor * right_factor + scale * right_sum
    return (new_first, new_second, new_left, new_right, update_sum.astype(jnp.bfloat16))


def solution(mesh):
    in_specs = (
        P(None, "mp", "dp"),
        P(None, "mp", "dp"),
        P(None, "mp", "dp"),
        P(None, "mp", "dp"),
        P(None, "mp", "dp"),
        P(None, "dp", "mp"),
        P(None, "mp", "dp"),
    )
    out_specs = (
        P(None, "mp", "dp"),
        P(None, "mp", "dp"),
        P(None, "mp", "dp"),
        P(None, "mp", "dp"),
        P(None, "mp", "dp"),
    )
    return jax.shard_map(
        per_device, mesh=mesh, in_specs=in_specs, out_specs=out_specs, check_vma=False
    )
```

profile of v0, /device:TPU:1, one launch (start us, length us, event | category | flops | bytes accessed | tf_op | source)
XLA Modules:
  0.0 453.0 jit_solution(4310972106720529222)
XLA Ops:
  7.2 0.0 all-gather.3.cloned.1.call-start
  7.2 1.0 copy.28
  8.2 1.6 pad_maximum_fusion
  9.8 0.0 all-gather.3.cloned.1.call-update
  9.9 0.0 all-gather.5.cloned.1.call-start
  9.9 1.7 pad_maximum_fusion.1
  11.6 0.0 all-gather.5.cloned.1.call-update
  11.6 99.2 %all-gather.3.cloned.1.call-done = bf16[4096,512]{1,0:T(8,128)(2,1)} async-done(((bf16[256,512]{1,0:T(8,128)(2,1)}), bf16[4096,512]{1,0:T(8,128)(2,1)}) %all-gather.3.cloned.1.call-update) | async-done | bytes 4194320 | tf_op jit(solution)/shard_map/all_gather | solution.py:21
  110.8 67.5 %all-gather.5.cloned.1.call-done = bf16[2,4096,256]{2,1,0:T(8,128)(2,1)} async-done(((bf16[2,256,256]{2,1,0:T(8,128)(2,1)}), bf16[2,4096,256]{2,1,0:T(8,128)(2,1)}) %all-gather.5.cloned.1.call-update) | async-done | bytes 4194320 | tf_op jit(solution)/shard_map/all_gather | solution.py:14
  178.3 3.0 fusion.28
  181.3 0.1 copy.29
  181.4 1.5 broadcast_in_dim.2
  182.9 6.9 %all-to-all-start = ((bf16[16,1,256,256]{2,3,1,0:T(8,128)(2,1)}), bf16[16,1,256,256]{2,3,1,0:T(8,128)(2,1)}, u32[]{:S(2)}, u32[]{:S(2)}) async-start(bf16[16,1,256,256]{2,3,1,0:T(8,128)(2,1)} %broadcast_in_dim.2), calls=%async_computation | async-start | bytes 4194304 | tf_op jit(solution)/shard_map/all_to_all | solution.py:37
  189.8 1.7 slice_bitcast_fusion.3
  191.5 25.0 %copy.45 = bf16[1,256,4096]{1,0,2:T(2,128)(2,1)} copy(bf16[1,256,4096]{1,2,0:T(8,128)(2,1)S(1)} %slice_bitcast_fusion.3) | data formatting | bytes 4194304 | tf_op jit(solution)/shard_map/transpose | solution.py:24
  216.6 0.5 broadcast.21
  217.1 21.6 %reduce.5 = bf16[4096,256]{1,0:T(8,128)(2,1)S(1)} reduce(bf16[4096,1,256]{2,1,0:T(2,128)(2,1)} %bitcast.92, bf16[]{:T(256)} %broadcast.21), dimensions={1}, to_apply=%bitcast.90.reduce_sub_computation | reduce | bytes 4194306
  238.7 2.1 reshape.85
  240.8 5.8 %all-to-all-start.2 = ((bf16[16,2,32768]{2,1,0:T(2,128)(2,1)}), bf16[16,2,32768]{2,1,0:T(2,128)(2,1)S(1)}, u32[]{:S(2)}, u32[]{:S(2)}) async-start(bf16[16,2,32768]{2,1,0:T(2,128)(2,1)} %reshape.85), calls=%async_computation.2 | async-start | bytes 4194304 | tf_op jit(solution)/shard_map/all_to_all | solution.py:63
  246.7 3.1 fusion.35
  249.8 0.0 copy-start.5
  249.8 0.0 copy-start.6
  249.8 0.3 copy-done
  250.1 2.1 convolution_convert_fusion.1
  252.2 22.9 %all-to-all-done.2 = bf16[16,2,32768]{2,1,0:T(2,128)(2,1)S(1)} async-done(((bf16[16,2,32768]{2,1,0:T(2,128)(2,1)}), bf16[16,2,32768]{2,1,0:T(2,128)(2,1)S(1)}, u32[]{:S(2)}, u32[]{:S(2)}) %all-to-all-start.2) | async-done | bytes 2097184 | tf_op jit(solution)/shard_map/all_to_all | solution.py:63
  275.1 5.3 %all-to-all-start.3 = ((bf16[16,1,256,256]{3,2,1,0:T(8,128)(2,1)}), bf16[16,1,256,256]{3,2,1,0:T(8,128)(2,1)}, u32[]{:S(2)}, u32[]{:S(2)}) async-start(bf16[16,1,256,256]{3,2,1,0:T(8,128)(2,1)} %bitcast.101), calls=%async_computation.3 | async-start | bytes 4194304 | tf_op jit(solution)/shard_map/all_to_all | solution.py:52
  280.4 1.6 slice-done
  282.0 25.0 %copy.46 = bf16[1,4096,256]{2,0,1:T(2,128)(2,1)} copy(bf16[1,4096,256]{2,1,0:T(8,128)(2,1)S(1)} %slice-done) | data formatting | bytes 4194304 | tf_op jit(solution)/shard_map/split | solution.py:15
  307.0 22.9 %reduce.4 = bf16[4096,256]{1,0:T(8,128)(2,1)} reduce(bf16[4096,1,256]{2,1,0:T(2,128)(2,1)} %bitcast.93, bf16[]{:T(256)} %broadcast.21), dimensions={1}, to_apply=%bitcast.91.reduce_sub_computation | reduce | bytes 4194306
  329.9 4.0 reshape.83
  333.9 7.2 %all-to-all-start.1 = ((bf16[16,2,32768]{2,1,0:T(2,128)(2,1)}), bf16[16,2,32768]{2,1,0:T(2,128)(2,1)}, u32[]{:S(2)}, u32[]{:S(2)}) async-start(bf16[16,2,32768]{2,1,0:T(2,128)(2,1)} %reshape.83), calls=%async_computation.1 | async-start | bytes 4194304 | tf_op jit(solution)/shard_map/all_to_all | solution.py:62
  341.1 1.9 reduce_sum.26
  343.0 2.3 convolution_convert_fusion
  345.4 0.6 copy.40
  346.0 2.1 copy.44
  348.1 41.9 %all-to-all-done.1 = bf16[16,2,32768]{2,1,0:T(2,128)(2,1)} async-done(((bf16[16,2,32768]{2,1,0:T(2,128)(2,1)}), bf16[16,2,32768]{2,1,0:T(2,128)(2,1)}, u32[]{:S(2)}, u32[]{:S(2)}) %all-to-all-start.1) | async-done | bytes 2097184 | tf_op jit(solution)/shard_map/all_to_all | solution.py:62
  390.0 5.4 %all-to-all-start.4 = ((bf16[16,1,256,256]{3,2,1,0:T(8,128)(2,1)}), bf16[16,1,256,256]{3,2,1,0:T(8,128)(2,1)}, u32[]{:S(2)}, u32[]{:S(2)}) async-start(bf16[16,1,256,256]{3,2,1,0:T(8,128)(2,1)} %bitcast.98), calls=%async_computation.4 | async-start | bytes 4194304 | tf_op jit(solution)/shard_map/all_to_all | solution.py:52
  395.4 6.8 %reshape.86 = bf16[4096,1,256]{2,1,0:T(2,128)(2,1)} reshape(bf16[16,2,32768]{2,1,0:T(2,128)(2,1)S(1)} %all-to-all-done.2) | data formatting | bytes 4194304
  402.2 2.5 copy.39
  404.8 0.0 copy-start.3
  404.8 2.5 copy.35
  407.3 3.7 fusion.25
  410.9 10.5 %reshape.84 = bf16[4096,1,256]{2,1,0:T(2,128)(2,1)} reshape(bf16[16,2,32768]{2,1,0:T(2,128)(2,1)} %all-to-all-done.1) | data formatting | bytes 4194304
  421.4 2.5 copy.38
  424.0 2.4 copy.33
  426.4 3.7 fusion.22
  430.1 13.5 %all-to-all-done.4 = bf16[16,1,256,256]{3,2,1,0:T(8,128)(2,1)} async-done(((bf16[16,1,256,256]{3,2,1,0:T(8,128)(2,1)}), bf16[16,1,256,256]{3,2,1,0:T(8,128)(2,1)}, u32[]{:S(2)}, u32[]{:S(2)}) %all-to-all-start.4) | async-done | bytes 2097184 | tf_op jit(solution)/shard_map/all_to_all | solution.py:52
  443.6 2.6 reduce_sum.27
  (13 shorter events, 0.0 us)
Async XLA Ops:
  7.2 103.7 %all-gather.3.cloned.1.call-start = ((), (), s32[]{:S(2)}) async-start(), calls=%async_computation.5 | async-start | bytes 4456448 | tf_op jit(solution)/shard_map/all_gather | solution.py:21
  9.9 168.4 %all-gather.5.cloned.1.call-start = ((), (), s32[]{:S(2)}) async-start(), calls=%async_computation.6 | async-start | bytes 4456448 | tf_op jit(solution)/shard_map/all_gather | solution.py:14
  182.9 57.9 %all-to-all-start = ((bf16[16,1,256,256]{2,3,1,0:T(8,128)(2,1)}), bf16[16,1,256,256]{2,3,1,0:T(8,128)(2,1)}, u32[]{:S(2)}, u32[]{:S(2)}) async-start(bf16[16,1,256,256]{2,3,1,0:T(8,128)(2,1)} %broadcast_in_dim.2), calls=%async_computation | async-start | bytes 4194304 | tf_op jit(solution)/shard_map/all_to_all | solution.py:37
  240.8 5.8 %copy-start.1 = (f32[1,256,256]{2,1,0:T(8,128)S(1)}, f32[1,256,256]{2,1,0:T(8,128)}, u32[]{:S(2)}) copy-start(f32[1,256,256]{2,1,0:T(8,128)} %param.9) | copy-start | bytes 786436
  240.8 5.8 %copy-start.2 = (f32[1,256,256]{2,1,0:T(8,128)S(1)}, f32[1,256,256]{2,1,0:T(8,128)}, u32[]{:S(2)}) copy-start(f32[1,256,256]{2,1,0:T(8,128)} %param.8) | copy-start | bytes 786436
  240.8 34.3 %all-to-all-start.2 = ((bf16[16,2,32768]{2,1,0:T(2,128)(2,1)}), bf16[16,2,32768]{2,1,0:T(2,128)(2,1)S(1)}, u32[]{:S(2)}, u32[]{:S(2)}) async-start(bf16[16,2,32768]{2,1,0:T(2,128)(2,1)} %reshape.85), calls=%async_computation.2 | async-start | bytes 4194304 | tf_op jit(solution)/shard_map/all_to_all | solution.py:63
  246.6 3.5 copy-start
  249.8 2.4 copy-start.5
  249.8 2.4 copy-start.6
  275.1 58.8 %all-to-all-start.3 = ((bf16[16,1,256,256]{3,2,1,0:T(8,128)(2,1)}), bf16[16,1,256,256]{3,2,1,0:T(8,128)(2,1)}, u32[]{:S(2)}, u32[]{:S(2)}) async-start(bf16[16,1,256,256]{3,2,1,0:T(8,128)(2,1)} %bitcast.101), calls=%async_computation.3 | async-start | bytes 4194304 | tf_op jit(solution)/shard_map/all_to_all | solution.py:52
  280.4 1.6 slice-start
  333.9 56.1 %all-to-all-start.1 = ((bf16[16,2,32768]{2,1,0:T(2,128)(2,1)}), bf16[16,2,32768]{2,1,0:T(2,128)(2,1)}, u32[]{:S(2)}, u32[]{:S(2)}) async-start(bf16[16,2,32768]{2,1,0:T(2,128)(2,1)} %reshape.83), calls=%async_computation.1 | async-start | bytes 4194304 | tf_op jit(solution)/shard_map/all_to_all | solution.py:62
  390.0 53.6 %all-to-all-start.4 = ((bf16[16,1,256,256]{3,2,1,0:T(8,128)(2,1)}), bf16[16,1,256,256]{3,2,1,0:T(8,128)(2,1)}, u32[]{:S(2)}, u32[]{:S(2)}) async-start(bf16[16,1,256,256]{3,2,1,0:T(8,128)(2,1)} %bitcast.98), calls=%async_computation.4 | async-start | bytes 4194304 | tf_op jit(solution)/shard_map/all_to_all | solution.py:52
  404.8 2.5 copy-start.3
  423.9 2.4 copy-start.4
Sparse Core Ops, SparseCore 0:
  10.3 100.4 all-gather.2
  114.2 64.0 all-gather.4
where the time goes:
time: 456 us; the launch traced here: 453 us
  waiting for transfers between devices  245 us (54%)
  local copies, waits for them, and re-layouts  92.9 us (20%)
  other arithmetic  52.3 us (11%)
  starting transfers between devices  30.7 us (7%)
  matrix products  17.8 us (4%)
  between operations  14.2 us (3%)
    all_gather x1, waiting for transfers between devices, turned_gather(): lax.all_gather(both, axis, axis=0, tiled=True)  99.2 us
    all_gather x1, waiting for transfers between devices, in_one_piece(): whole = lax.all_gather(both, axis, axis=dim, tiled=True)  67.5 us
    unnamed x2, other arithmetic  44.5 us
    all_to_all x1, waiting for transfers between devices, per_device(): lax.all_to_all(column_grad, 'dp', split_axis=1, concat_axis=2, tiled=True)  41.9 us
    unnamed x23, local copies, waits for them, and re-layouts  31 us
    transpose x2, local copies, waits for them, and re-layouts, turned_gather(): gathered.append(jnp.moveaxis(section, 0, dim))  26.8 us
    split x3, local copies, waits for them, and re-layouts, in_one_piece(): jnp.split(whole, [sum(widths[:k]) for k in range(1, len(widths))], axis=a...  26.6 us
    all_to_all x1, waiting for transfers between devices, per_device(): lax.all_to_all(row_grad, 'mp', split_axis=2, concat_axis=1, tiled=True)  22.9 us
  transfers between devices with their start and end apart: 7, of which 5 were waited for; matrix products, arithmetic and copies ran while one was open for 33% of the time, Pallas kernels for 0%

commit v1 on v0

v1 whole, which is shorter than its diff:
```python
import jax
import jax.numpy as jnp
from jax import lax
from jax.experimental import pallas as pl
from jax.experimental.pallas import tpu as pltpu
from jax.sharding import PartitionSpec as P

decay_moment = 0.95
decay_factor = 0.95
epsilon = 1e-08
N = 256
H = N // 2
NZ = 8
NX = 4
NSEM = 400

BF = jnp.bfloat16
F32 = jnp.float32


def dot(a, b):
    return jnp.dot(a, b, preferred_element_type=F32)


def turned(a):
    return a.astype(F32).T


class Place:
    def __init__(self):
        self.j = lax.axis_index("dp")
        self.i = lax.axis_index("mp")
        self.z, self.yl = self.j // 2, self.j % 2
        self.yh, self.x, self.c = self.i // 8, (self.i // 2) % NX, self.i % 2

    def device(self, dz=0, dy=0, dh=0, dx=0, dc=0):
        return {"dp": self.dp(dz, dy), "mp": self.mp(dh, dx, dc)}

    def dp(self, dz=0, dy=0):
        yl = 1 - self.yl if dy else self.yl
        return lax.rem(self.z + dz + NZ, NZ) * 2 + yl

    def mp(self, dh=0, dx=0, dc=0):
        yh = 1 - self.yh if dh else self.yh
        c = 1 - self.c if dc else self.c
        return yh * 8 + lax.rem(self.x + dx + NX, NX) * 2 + c


class Wires:
    def __init__(self, send_sem, recv_sem):
        self.send_sem, self.recv_sem = send_sem, recv_sem
        self.count = 0
        self.sent = []

    def send(self, src, dst, device):
        k = self.count
        self.count += 1
        assert k < NSEM
        copy = pltpu.make_async_remote_copy(
            src_ref=src,
            dst_ref=dst,
            send_sem=self.send_sem.at[k],
            recv_sem=self.recv_sem.at[k],
            device_id=device,
            device_id_type=pl.DeviceIdType.MESH,
        )
        copy.start()
        self.sent.append(copy)
        return copy

    def drain(self):
        for copy in self.sent:
            copy.wait_send()


TOP, BOTTOM = pl.ds(0, H), pl.ds(H, H)
WAYS = ((1, TOP), (-1, BOTTOM))


def gather_dp(w, p, own, buf, t):
    got = {}

    def start():
        for way, _ in WAYS:
            got["A", 1, way] = w.send(own, buf.at[p.j], p.device(dz=way))
        got["B", 0] = w.send(own, buf.at[p.j], p.device(dy=1))

    def pass_a(s):
        def run():
            for way, half in WAYS:
                got["A", s, way].wait_recv()
                block = buf.at[p.dp(-s * way)]
                if s < 3:
                    got["A", s + 1, way] = w.send(block, block, p.device(dz=way))
                else:
                    part = block.at[half]
                    got["A", 4, way] = w.send(part, part, p.device(dz=way))
                    got["F", 3, way] = w.send(block, block, p.device(dy=1))

        return run

    def pass_b(s):
        def run():
            if s == 0:
                got["B", 0].wait_recv()
            for way, _ in WAYS:
                if s > 0:
                    got["B", s, way].wait_recv()
                block = buf.at[p.dp(-s * way, 1)]
                if s < 2:
                    got["B", s + 1, way] = w.send(block, block, p.device(dz=way))

        return run

    def pass_far():
        for way, half in WAYS:
            got["A", 4, way].wait_recv()
            part = buf.at[p.dp(4)].at[half]
            got["F", 4, way] = w.send(part, part, p.device(dy=1))

    def last(s):
        def run():
            for way, _ in WAYS:
                got["F", s, way].wait_recv()

        return run

    steps = (start, pass_a(1), pass_b(0), pass_a(2), pass_b(1), pass_a(3), pass_b(2), pass_far, last(3), last(4))
    return list(zip(t, steps))


def gather_mp(w, p, own, buf, t):
    got = {}

    def over(key, ref):
        got["C", key] = w.send(ref, ref, p.device(dc=1))

    def start():
        got["C", "own"] = w.send(own, buf.at[p.i], p.device(dc=1))
        got["B", 0] = w.send(own, buf.at[p.i], p.device(dh=1))
        for way, _ in WAYS:
            got["A", 1, way] = w.send(own, buf.at[p.i], p.device(dx=way))

    def near(name, h):
        def run():
            for way, half in WAYS:
                got[name, 1, way].wait_recv()
                block = buf.at[p.mp(h, -way)]
                part = block.at[half]
                got[name, 2, way] = w.send(part, part, p.device(dx=way))
                over((name, 1, way), block)

        return run

    def partner():
        got["B", 0].wait_recv()
        block = buf.at[p.mp(1)]
        for way, _ in WAYS:
            got["B", 1, way] = w.send(block, block, p.device(dx=way))
        over(("B", 0), block)

    def far(name, h):
        def run():
            for way, half in WAYS:
                got[name, 2, way].wait_recv()
                over((name, 2, way), buf.at[p.mp(h, 2)].at[half])

        return run

    def siblings():
        for key in list(got):
            if key[0] == "C":
                got[key].wait_recv()

    steps = (start, near("A", 0), partner, far("A", 0), near("B", 1), far("B", 1), siblings)
    return list(zip(t, steps))


def scatter_mp(w, p, term, done, bufs, t):
    send_c, got_c, send_x, got_x = bufs
    got = {}
    sides = ((1, 1), (0, 0))

    def start():
        for k in range(8):
            yh, x = k // 4, k % 4
            send_c[k] = term(p.mp(yh, x, 1)).astype(BF)
            got["C", k] = w.send(send_c.at[k], got_c.at[k], p.device(dc=1))

    def chip(h, dx):
        k = h * 4 + dx % 4
        return term(p.mp(h, dx)) + got_c[k].astype(F32)

    def far():
        for k in range(8):
            got["C", k].wait_recv()
        for h, s in sides:
            send_x[3 * s] = chip(h, 2).astype(BF)
            for way, half in WAYS:
                part = send_x.at[3 * s].at[half]
                got["far", h, way] = w.send(part, got_x.at[3 * s].at[half], p.device(dx=way))

    def near():
        for h, s in sides:
            for n, (way, half) in enumerate(WAYS):
                slot = 3 * s + 1 + n
                total = chip(h, way)
                got["far", h, way].wait_recv()
                low = got_x[3 * s, half].astype(F32)
                send_x[slot] = total.astype(BF)
                send_x[slot, half] = (total[half.start : half.start + H] + low).astype(BF)
                got["near", h, way] = w.send(send_x.at[slot], got_x.at[slot], p.device(dx=way))

    def arrived(h):
        total = chip(h, 0)
        for n, (way, _) in enumerate(WAYS):
            got["near", h, way].wait_recv()
            total = total + got_x[3 * h + 1 + n].astype(F32)
        return total

    def partner():
        send_x[6] = arrived(1).astype(BF)
        got["y"] = w.send(send_x.at[6], got_x.at[6], p.device(dh=1))

    def finish():
        total = arrived(0)
        got["y"].wait_recv()
        done(total + got_x[6].astype(F32))

    return list(zip(t, (start, far, near, partner, finish)))


def scatter_dp(w, p, term, done, bufs, t):
    send, got_ref = bufs
    got = {}

    def put(slot, value, device):
        send[slot] = value.astype(BF)
        got[slot] = w.send(send.at[slot], got_ref.at[slot], device)

    def take(slot):
        got[slot].wait_recv()
        return got_ref[slot].astype(F32)

    def start():
        put(12, term(p.dp(4, 1)), p.device(dy=1))
        for n, (way, _) in enumerate(WAYS):
            put(7 + n, term(p.dp(2 * way, 1)), p.device(dz=way))
        for n, (way, _) in enumerate(WAYS):
            put(13 + n, term(p.dp(3 * way, 1)), p.device(dy=1))

    def a4():
        send[0] = (term(p.dp(4)) + take(12)).astype(BF)
        for way, half in WAYS:
            got["half", way] = w.send(send.at[0].at[half], got_ref.at[0].at[half], p.device(dz=way))

    def b1():
        for n, (way, _) in enumerate(WAYS):
            put(9 + n, term(p.dp(way, 1)) + take(7 + n), p.device(dz=way))

    def a3():
        for n, (way, half) in enumerate(WAYS):
            total = term(p.dp(3 * way)) + take(13 + n)
            got["half", way].wait_recv()
            low = got_ref[0, half].astype(F32)
            send[1 + n] = total.astype(BF)
            send[1 + n, half] = (total[half.start : half.start + H] + low).astype(BF)
            got[1 + n] = w.send(send.at[1 + n], got_ref.at[1 + n], p.device(dz=way))

    def a2():
        for n, (way, _) in enumerate(WAYS):
            put(3 + n, term(p.dp(2 * way)) + take(1 + n), p.device(dz=way))

    def b0():
        put(11, term(p.dp(0, 1)) + take(9) + take(10), p.device(dy=1))

    def a1():
        for n, (way, _) in enumerate(WAYS):
            put(5 + n, term(p.dp(way)) + take(3 + n), p.device(dz=way))

    def finish():
        done(term(p.dp(0)) + take(11) + take(5) + take(6))

    return list(zip(t, (start, a4, b1, a3, a2, b0, a1, finish)))


def kernel(
    g, m1, m2, lf, rf, ql, qr,
    o_m1, o_m2, o_l, o_r, o_u,
    gb, qlb, qrb, tb, gtb,
    g_turned, ql_turned, t_own, d_turned, back,
    acc_t, acc_rot, acc_l,
    cs_b, cg_b, xs_b, xg_b, cs_r, cg_r, xs_r, xg_r, zs, zg,
    send_sem, recv_sem,
):
    p = Place()
    w = Wires(send_sem, recv_sem)
    across = {"dp": p.i, "mp": p.j}
    apart = p.i != p.j
    peers = [p.device(dz=1), p.device(dz=-1), p.device(dy=1), p.device(dh=1), p.device(dx=1), p.device(dx=-1), p.device(dc=1)]

    barrier = pltpu.get_barrier_semaphore()
    for peer in peers:
        pl.semaphore_signal(barrier, inc=1, device_id=peer, device_id_type=pl.DeviceIdType.MESH)

    @pl.when(apart)
    def _():
        pl.semaphore_signal(barrier, inc=1, device_id=across, device_id_type=pl.DeviceIdType.MESH)

    pl.semaphore_wait(barrier, jnp.where(apart, 8, 7))

    turn = pltpu.make_async_remote_copy(
        src_ref=g_turned,
        dst_ref=gtb.at[p.j],
        send_sem=send_sem.at[NSEM],
        recv_sem=recv_sem.at[NSEM],
        device_id=across,
        device_id_type=pl.DeviceIdType.MESH,
    )

    def prepare():
        g_turned[...] = turned(g[...]).astype(BF)

        @pl.when(apart)
        def _():
            turn.start()

        @pl.when(jnp.logical_not(apart))
        def _():
            gtb[p.i] = g_turned[...]

        gb[p.j] = g[...]
        qrb[p.i] = qr[...]
        ql_turned[...] = turned(ql[...]).astype(BF)
        qlb[p.j] = ql_turned[...]

    def turn_arrived():
        @pl.when(apart)
        def _():
            turn.wait()

    def product_t(first, count, fresh):
        def run():
            if fresh:
                acc_t[...] = jnp.zeros_like(acc_t)

            def body(n, _):
                k = lax.rem(p.z + first + n // 2, NZ) * 2 + n % 2
                acc_t[...] += dot(gb[k], qrb[k])
                return 0

            lax.fori_loop(0, count, body, 0)
            if not fresh:
                t_own[...] = acc_t[...].astype(BF)
                tb[p.i] = t_own[...]

        return run

    def product_l():
        acc_l[...] = jnp.zeros_like(acc_l)

        def body(k, _):
            acc_l[...] += dot(gb[k], gtb[k])
            return 0

        lax.fori_loop(0, 16, body, 0)
        o_l[...] = decay_factor * lf[...] + (1.0 - decay_factor) * acc_l[...]

    def moments():
        acc_rot[...] = jnp.zeros_like(acc_rot)

        def body(k, _):
            acc_rot[...] += dot(qlb[k], tb[k])
            return 0

        lax.fori_loop(0, 16, body, 0)
        rotated = acc_rot[...]
        first = decay_moment * m1[...] + (1.0 - decay_moment) * rotated
        second = decay_moment * m2[...] + (1.0 - decay_moment) * rotated * rotated
        o_m1[...] = first
        o_m2[...] = second
        direction = (first / (jnp.sqrt(second) + epsilon)).astype(BF)
        d_turned[...] = turned(direction).astype(BF)

    def back_done(total):
        back[...] = total.astype(BF)

    def right_done(total):
        o_r[...] = decay_factor * rf[...] + (1.0 - decay_factor) * total.T

    def update_done(total):
        o_u[...] = total.T.astype(BF)

    def back_term(k):
        return dot(d_turned[...], qlb[k])

    def right_term(k):
        return dot(g_turned[...], gb[k])

    def update_term(k):
        return dot(qrb[k], back[...])

    plan = []
    plan += gather_dp(w, p, g, gb, (0, 4.8, 4.9, 10, 12, 15, 18, 19, 20, 23))
    plan += gather_mp(w, p, qr, qrb, (0.1, 4.95, 6, 9, 10.5, 13.5, 14.5))
    plan += [(0.2, prepare), (7.9, turn_arrived)]
    plan += gather_dp(w, p, ql_turned, qlb, (0.3, 15.2, 15.3, 22, 23.8, 28, 29, 31, 32, 34))
    plan += gather_mp(w, p, gtb.at[p.i], gtb, (8, 14, 15.1, 19.1, 19.5, 22.5, 23.5))
    plan += [(18.5, product_t(6, 10, True)), (23.6, product_t(3, 6, False))]
    plan += gather_mp(w, p, t_own, tb, (23.7, 28.5, 29.5, 32.5, 33, 36.5, 37.5))
    plan += [(25, product_l), (38, moments)]
    plan += scatter_mp(w, p, back_term, back_done, (cs_b, cg_b, xs_b, xg_b), (39, 42, 45.5, 51, 55))
    plan += scatter_dp(w, p, update_term, update_done, (zs, zg), (56, 61, 61.5, 64.5, 69, 70, 74, 79))
    plan += scatter_mp(w, p, right_term, right_done, (cs_r, cg_r, xs_r, xg_r), (26, 57, 62, 67, 71))
    for _, step in sorted(plan, key=lambda item: item[0]):
        step()
    w.drain()


def per_device(gradient, first_moment, second_moment, left_factor, right_factor, left_basis, right_basis):
    ins = [a.reshape(N, N) for a in (gradient, first_moment, second_moment, left_factor, right_factor, left_basis, right_basis)]
    vmem = pl.BlockSpec(memory_space=pltpu.VMEM)
    block = pltpu.VMEM((N, N), BF)
    wide = pltpu.VMEM((N, N), F32)
    whole = pltpu.VMEM((16, N, N), BF)
    scatter = [pltpu.VMEM((8, N, N), BF)] * 2 + [pltpu.VMEM((7, N, N), BF)] * 2
    outs = pl.pallas_call(
        kernel,
        name="soap",
        out_shape=[jax.ShapeDtypeStruct((N, N), F32)] * 4 + [jax.ShapeDtypeStruct((N, N), BF)],
        in_specs=[vmem] * 7,
        out_specs=[vmem] * 5,
        scratch_shapes=[whole] * 5
        + [block] * 5
        + [wide] * 3
        + scatter * 2
        + [pltpu.VMEM((15, N, N), BF)] * 2
        + [pltpu.SemaphoreType.DMA((NSEM + 1,))] * 2,
        compiler_params=pltpu.CompilerParams(collective_id=0, has_side_effects=True, vmem_limit_bytes=60 * 1024 * 1024),
    )(*ins)
    return tuple(o.reshape(1, N, N) for o in outs)


def solution(mesh):
    spec = P(None, "mp", "dp")
    return jax.shard_map(
        per_device,
        mesh=mesh,
        in_specs=(spec,) * 5 + (P(None, "dp", "mp"), spec),
        out_specs=(spec,) * 5,
        check_vma=False,
    )
```

time: 456 us -> 125 us (0.27)
  the two profiles are of different devices: /device:TPU:1 before, /device:TPU:32 now
where the time goes in v1:
time: 125 us
  Pallas kernels  119 us (95%)
  local copies, waits for them, and re-layouts  5.45 us (4%)
    pallas_call x1, Pallas kernels, per_device(): pl.pallas_call(kernel, name='soap', out_shape=[jax.ShapeDtypeStruct((N, N...  119 us
    unnamed x13, local copies, waits for them, and re-layouts  5.45 us

profile of v1, /device:TPU:32, one launch (start us, length us, event | category | flops | bytes accessed | tf_op | source)
XLA Modules:
  0.0 124.8 jit_solution(4634140195993690417)
XLA Ops:
  0.6 118.7 %soap.1 = (f32[256,256]{1,0:T(8,128)}, f32[256,256]{1,0:T(8,128)}, f32[256,256]{1,0:T(8,128)}, f32[256,256]{1,0:T(8,128)}, bf16[256,256]{1,0:T(8,128)(2,1)}) custom-call(bf16[256,256]{1,0:T(8,128)(2,1)} %bitcast.21, f32[256,256]{1,0:T(8,128)} %bitcast.16, f32[256,256]{1,0:T(8,128)} %bitcast.17, f32[256,256]{1,0:T(8,128)} %bitcast.18, f32[256,256]{1,0:T(8,128)} %bitcast.19, ...), custom_call_target="tpu_custom_call" | custom-call | tf_op jit(solution)/shard_map/soap/pallas_call | solution.py:427
  119.3 0.0 copy-start.2
  119.4 1.7 %copy.17 = f32[1,256,256]{2,1,0:T(8,128)} copy(f32[1,256,256]{2,1,0:T(8,128)} %bitcast.15) | data formatting | bytes 524288
  121.1 0.0 copy-done.2
  121.1 0.0 copy-start.1
  121.1 0.7 copy.18
  121.8 0.3 copy-done.1
  122.1 0.0 copy-start
  122.1 0.7 copy.19
  122.8 0.3 copy-done
  123.2 0.0 copy-start.3
  123.2 0.7 copy.20
  123.9 0.3 copy-done.3
  124.2 0.7 copy.21
Async XLA Ops:
  119.3 1.7 %copy-start.2 = (f32[256,256]{1,0:T(8,128)S(1)}, f32[256,256]{1,0:T(8,128)}, u32[]{:S(2)}) copy-start(f32[256,256]{1,0:T(8,128)} %get-tuple-element.11) | copy-start | bytes 786436
  121.1 1.0 copy-start.1
  122.1 1.0 copy-start
  123.2 1.0 copy-start.3

commit v2 on v0

v2 whole, which is shorter than its diff:
```python
import jax
import jax.numpy as jnp
from jax import lax
from jax.experimental import pallas as pl
from jax.experimental.pallas import tpu as pltpu
from jax.sharding import PartitionSpec as P

decay_moment = 0.95
decay_factor = 0.95
epsilon = 1e-08
N = 256
NZ = 8
NX = 4
NY = 4
NSEND = 19
NRECV = 133

BF = jnp.bfloat16
F32 = jnp.float32
MESH = pl.DeviceIdType.MESH
TIMES = {
    "mi": (0.00,),
    "hg": (0.02,),
    "hq": (1.54,),
    "hl": (2.18,),
    "mm": (34.45,),
    "hm": (34.67,),
    "gz": (2.12, 5.13, 5.87, 6.54, 7.24, 8.15, 8.88, 9.58, 10.29, 11.16, 11.89, 12.60, 13.30, 14.17, 14.90, 15.60, 16.31, 11.46, 17.45,),
    "qp": (2.06, 5.79, 7.19, 8.81, 11.62, 13.73, 12.33, 17.95, 18.65,),
    "lz": (16.00, 20.04, 20.08, 20.42, 21.12, 23.06, 23.79, 24.46, 25.17, 26.07, 26.80, 27.51, 28.21, 29.08, 29.81, 30.51, 31.22, 26.35, 32.30,),
    "t": (18.67, 19.39,),
    "tp": (19.98, 23.71, 25.12, 27.23, 30.04, 32.15, 30.74, 34.96, 35.66,),
    "r": (32.32, 35.68, 36.32,),
    "b0": (36.57, 37.12, 40.22, 40.92, 43.38, 41.33, 48.66, 51.74,),
    "b1": (37.59, 38.14, 41.65, 42.33, 46.20, 42.68, 49.01, 52.72,),
    "u0": (51.82, 52.16, 52.39, 53.70, 53.98, 54.44, 53.77, 53.82, 56.80, 56.86, 59.85, 60.55, 62.89, 63.59, 65.93, 66.64,),
    "u1": (52.80, 53.14, 53.37, 54.94, 55.26, 55.75, 55.06, 55.00, 58.21, 58.27, 61.25, 61.96, 64.30, 65.00, 67.34, 68.04,),
    "gp": (10.99, 15.92, 32.96, 22.38, 29.41, 33.63, 38.61, 33.55, 38.63,),
    "ls": (38.65, 38.99, 39.22, 41.04, 41.60, 42.58, 41.11, 41.22, 41.16, 41.27, 44.15, 44.85, 44.21, 44.91, 47.19, 48.60, 47.89, 50.44, 50.50, 51.64, 50.94, 54.03, 54.19, 55.59, 54.89, 57.56,),
    "rp": (49.27, 49.92, 53.88, 54.55, 57.66, 55.31, 63.99, 67.77,),
    "rr": (46.61,),
    "rl": (57.61,),
    "rt": (67.85,),
    "ru": (68.09,),
}


def dot(a, b):
    return jnp.dot(a, b, preferred_element_type=F32)


def turned(a):
    return a.astype(F32).T


class Place:
    def __init__(self):
        j, i = lax.axis_index("dp"), lax.axis_index("mp")
        self.z, self.y = j // 2, (i // 8) * 2 + j % 2
        self.x, self.c = (i // 2) % NX, i % 2
        self.away = j % 2 != self.c

    def row(self, dy=0, dx=0):
        y = lax.rem(self.y + dy + NY, NY)
        return (y // 2) * 8 + lax.rem(self.x + dx + NX, NX) * 2 + y % 2

    def column(self, dz=0, dc=0):
        return lax.rem(self.z + dz + NZ, NZ) * 2 + (1 - self.c if dc else self.c)

    def device(self, dz=0, dy=0, dx=0, dc=0):
        y = lax.rem(self.y + dy + NY, NY)
        c = 1 - self.c if dc else self.c
        z, x = lax.rem(self.z + dz + NZ, NZ), lax.rem(self.x + dx + NX, NX)
        return {"dp": z * 2 + y % 2, "mp": (y // 2) * 8 + x * 2 + c}

    def twin(self):
        y = self.y + 1 - 2 * (self.y % 2)
        return {"dp": self.z * 2 + y % 2, "mp": (y // 2) * 8 + self.x * 2 + 1 - self.c}


class Wires:
    def __init__(self, send_sem, recv_sem):
        self.send_sem, self.recv_sem = send_sem, recv_sem
        self.sends = self.recvs = 0

    def flow(self, gauge):
        self.sends += 1
        assert self.sends <= NSEND
        return Flow(self, self.send_sem.at[self.sends - 1], gauge)

    def receiver(self):
        self.recvs += 1
        assert self.recvs <= NRECV
        return self.recv_sem.at[self.recvs - 1]


class Flow:
    def __init__(self, wires, send_sem, gauge):
        self.wires, self.send_sem, self.gauge = wires, send_sem, gauge
        self.groups = {}

    def send(self, group, src, dst, device):
        if group not in self.groups:
            self.groups[group] = self.wires.receiver()
        pltpu.make_async_remote_copy(
            src_ref=src,
            dst_ref=dst,
            send_sem=self.send_sem,
            recv_sem=self.groups[group],
            device_id=device,
            device_id_type=MESH,
        ).start()

    def pause(self, sem, quarters):
        if quarters >= 4:
            assert quarters % 4 == 0
            size = self.gauge.at[pl.ds(0, quarters // 4)]
        else:
            size = self.gauge.at[0, pl.ds(0, quarters * 64)]
        pltpu.make_async_copy(size, size, sem).wait()

    def wait(self, group, quarters):
        self.pause(self.groups[group], quarters)

    def drain(self):
        self.pause(self.send_sem, 60)


WAYS = (1, -1)


def half(f):
    return pl.ds(f * 128, 128)


def quarter(f, way):
    return pl.ds(f * 128 + (0 if way == 1 else 64), 64)


def part(h):
    return pl.ds(h * 64, 64)


def along(f, a=0, b=0):
    return {"dy": a, "dx": b} if f == 0 else {"dy": b, "dx": a}


def gather_z(w, p, own, buf):
    def start():
        for h in range(4):
            for way in WAYS:
                w.send((1, h), own.at[part(h)], buf.at[p.column(), part(h)], p.device(dz=way))
        w.send("C near", own, buf.at[p.column()], p.device(dc=1))

    def arrive(n, h):
        last = WAYS[h // 2]

        def step():
            w.wait((n, h), 2 if n < 4 else 1)
            for way in WAYS if n < 4 else (last,):
                ref = buf.at[p.column(-n * way), part(h)]
                if n < 3 or (n == 3 and way == last):
                    w.send((n + 1, h), ref, ref, p.device(dz=way))
            for way in WAYS if n < 4 else (last,):
                ref = buf.at[p.column(-n * way), part(h)]
                w.send("C near" if n < 3 else "C far", ref, ref, p.device(dc=1))

        return step

    def near_siblings():
        w.wait("C near", 4 * 5)

    def far_siblings():
        w.wait("C far", 4 * 3)

    return [start] + [arrive(n, h) for n in (1, 2, 3, 4) for h in range(4)] + [near_siblings, far_siblings]


def gather_plane(w, p, own, buf):
    def send(group, f, ref, dst=None, **to):
        w.send(group, ref, ref if dst is None else dst, p.device(**along(f, **to)))

    def block(f, a, b, rows):
        return buf.at[p.row(**along(f, a, b)), rows]

    def start():
        for stage in ("a", "b"):
            for f in (0, 1):
                for way in WAYS:
                    dst = buf.at[p.row(), half(f)]
                    if stage == "a":
                        send("a1", f, own.at[half(f)], dst, a=way)
                    else:
                        send(("b", 0), f, own.at[half(f)], dst, b=way)

    def first():
        w.wait("a1", 8)
        for f in (0, 1):
            for way in WAYS:
                send("a2", f, block(f, -way, 0, quarter(f, way)), a=way)
        for f in (0, 1):
            for way in WAYS:
                for v in WAYS:
                    send(("b", 1), f, block(f, -way, 0, half(f)), b=v)

    def second(q):
        def step():
            w.wait(("b", q), 8 if q != 1 else 16)
            for r in (1, -1) if q == 1 else (q,):
                for f in (0, 1):
                    for v in WAYS:
                        send(("bb", q), f, block(f, r, -v, quarter(f, v)), b=v)

        return step

    def opposite():
        w.wait("a2", 4)
        for f in (0, 1):
            for v in WAYS:
                send(("b", 2), f, block(f, 2, 0, half(f)), b=v)

    def last(q):
        def step():
            w.wait(("bb", q), 4 if q != 1 else 8)

        return step

    return [start, first, second(0), opposite, second(1), second(2), last(0), last(1), last(2)]


def scatter_plane(w, p, term, done, bufs):
    base, out, into = bufs
    early = [(dy, dx) for dy in range(4) for dx in range(4) if dy == 2 or dx == 2]
    late = [(dy, dx) for dy in range(4) for dx in range(4) if dy != 2 and dx != 2]

    def terms(places):
        for dy, dx in places:
            base[dy * 4 + dx] = term(p.row(dy, dx))

    def held(f, a, b, rows):
        d = along(f, a, b)
        return base[(d["dy"] % 4) * 4 + d["dx"] % 4, rows]

    def send(group, f, slot, rows, **to):
        w.send(group, out.at[slot, rows], into.at[slot, rows], p.device(**along(f, **to)))

    def far():
        terms(early)
        for q in (2, 1, -1, 0):
            for f in (0, 1):
                out[q % 4, half(f)] = held(f, q, 2, half(f)).astype(BF)
        for q in (2, 1, -1, 0):
            for f in (0, 1):
                for v in WAYS:
                    send((2, abs(q)), f, q % 4, quarter(f, v), b=v)

    def rest():
        terms(late)

    def near(q):
        def step():
            w.wait((2, q), 4 if q != 1 else 8)
            for r in (1, -1) if q == 1 else (q,):
                for f in (0, 1):
                    for n, v in enumerate(WAYS):
                        slot, rows = 4 + (r % 4) * 2 + n, quarter(f, v)
                        out[slot, half(f)] = held(f, r, v, half(f)).astype(BF)
                        out[slot, rows] = (held(f, r, v, rows) + into[r % 4, rows].astype(F32)).astype(BF)
                        send((1, q), f, slot, half(f), b=v)

        return step

    def line(f, q, rows):
        total = held(f, q, 0, rows)
        for n, v in enumerate(WAYS):
            total = total + into[4 + (q % 4) * 2 + n, rows].astype(F32)
        return total

    def opposite():
        w.wait((1, 2), 8)
        for f in (0, 1):
            out[12, half(f)] = line(f, 2, half(f)).astype(BF)
            for way in WAYS:
                send("a2", f, 12, quarter(f, way), a=way)

    def beside():
        w.wait((1, 1), 16)
        w.wait("a2", 4)
        for f in (0, 1):
            for n, way in enumerate(WAYS):
                rows = quarter(f, way)
                out[13 + n, half(f)] = line(f, way, half(f)).astype(BF)
                out[13 + n, rows] = (line(f, way, rows) + into[12, rows].astype(F32)).astype(BF)
                send("a1", f, 13 + n, half(f), a=way)

    def finish():
        w.wait((1, 0), 8)
        w.wait("a1", 8)
        for f in (0, 1):
            total = line(f, 0, half(f))
            for n in (0, 1):
                total = total + into[13 + n, half(f)].astype(F32)
            done(f, total)

    return [far, rest, near(2), near(1), opposite, near(0), beside, finish]


def scatter_z(w, p, term, done, bufs, parts=2):
    base, mate_out, mate_in, out, into = bufs
    stages = ((4, 3, 5), (2, 6), (1, 7, 0))
    size = N // parts

    def rows(h):
        return pl.ds(h * size, size)

    def slot(n, way):
        return 0 if n == 4 else 1 + (n - 1) * 2 + (0 if way == 1 else 1)

    def start(k):
        def step():
            for dz in stages[k]:
                mate_out[dz] = term(p.column(dz, 1)).astype(BF)
            for dz in stages[k]:
                w.send(("C", k), mate_out.at[dz], mate_in.at[dz], p.device(dc=1))
            for dz in stages[k]:
                base[dz] = term(p.column(dz))

        return step

    def chip(k):
        def step():
            w.wait(("C", k), 4 * len(stages[k]))
            for dz in stages[k]:
                base[dz] = base[dz] + mate_in[dz].astype(F32)

        return step

    def push(n, h):
        last = WAYS[h // (parts // 2)]

        def step():
            if n < 3:
                w.wait((n + 1, h), 8 // parts)
            if n == 3:
                w.wait((4, h), 4 // parts)
            for way in WAYS if n < 4 else (last,):
                total = base[(n * way) % 8, rows(h)]
                if n < 3 or (n == 3 and way == last):
                    total = total + into[slot(n + 1, way), rows(h)].astype(F32)
                out[slot(n, way), rows(h)] = total.astype(BF)
                w.send((n, h), out.at[slot(n, way), rows(h)], into.at[slot(n, way), rows(h)], p.device(dz=way))

        return step

    def finish(h):
        def step():
            w.wait((1, h), 8 // parts)
            total = base[0, rows(h)]
            for way in WAYS:
                total = total + into[slot(1, way), rows(h)].astype(F32)
            done(rows(h), total)

        return step

    steps = [start(0), start(1), start(2), chip(0), chip(1), chip(2)]
    return steps + [push(n, h) for n in (4, 3, 2, 1) for h in range(parts)] + [finish(h) for h in range(parts)]


def kernel(
    g_in, m1_in, m2_in, ql_in, qr_in,
    o_rot, o_l, o_r, o_u,
    g_0, ql_0, qr_0, m1_0, m2_0, mm_0, mm,
    g, ql, qr,
    gb, qlb, qrb, tb, gcb,
    g_turned, ql_turned, t_own, d_turned, u_0, u_1,
    left, left_1, right, right_1, rot_0, rot_1,
    acc_t, rot, right_sum,
    back_0, back_1,
    pb_0, po_0, pi_0, pb_1, po_1, pi_1, pb_r, po_r, pi_r,
    zb_0, zmo_0, zmi_0, zo_0, zi_0, zb_1, zmo_1, zmi_1, zo_1, zi_1, zb_l, zmo_l, zmi_l, zo_l, zi_l,
    send_sem, recv_sem, load_sem,
):
    p = Place()
    w = Wires(send_sem, recv_sem)
    home = jnp.logical_not(p.away)
    peers = [p.device(dz=1), p.device(dz=-1), p.device(dy=1), p.device(dy=-1), p.device(dx=1), p.device(dx=-1), p.device(dc=1), p.twin()]

    barrier = pltpu.get_barrier_semaphore()
    for peer in peers:
        pl.semaphore_signal(barrier, inc=1, device_id=peer, device_id_type=MESH)

    loads = {}
    for n, (name, src, dst) in enumerate((("g", g_in, g_0), ("qr", qr_in, qr_0), ("ql", ql_in, ql_0), ("m1", m1_in, m1_0), ("m2", m2_in, m2_0))):
        loads[name] = pltpu.make_async_copy(src, dst, load_sem.at[n])
        loads[name].start()
    loads["g"].wait()
    loads["qr"].wait()
    pl.semaphore_wait(barrier, 8)

    moves = {}

    def move(name, src, dst):
        copy = pltpu.make_async_remote_copy(
            src_ref=src,
            dst_ref=dst,
            send_sem=w.flow(None).send_sem,
            recv_sem=w.receiver(),
            device_id=p.twin(),
            device_id_type=MESH,
        )
        moves[name] = copy

        @pl.when(p.away)
        def _():
            copy.start()

        @pl.when(home)
        def _():
            dst[...] = src[...]

    def moved(name):
        @pl.when(p.away)
        def _():
            moves[name].wait_recv()

    def move_in():
        move("g", g_0, g)
        move("qr", qr_0, qr)
        loads["ql"].wait()
        move("ql", ql_0, ql)

    def have_g():
        moved("g")

    def have_qr():
        moved("qr")

    def have_ql():
        gb[p.column()] = g[...]
        gcb[p.row()] = g[...]
        qrb[p.row()] = qr[...]
        moved("ql")
        ql_turned[...] = turned(ql[...]).astype(BF)
        qlb[p.column()] = ql_turned[...]

    def move_moments():
        loads["m1"].wait()
        loads["m2"].wait()
        mm_0[0] = m1_0[...].astype(BF)
        mm_0[1] = m2_0[...].astype(BF)
        move("m", mm_0, mm)
        g_turned[...] = turned(g[...]).astype(BF)

    def have_moments():
        moved("m")

    def gathered(acc, lefts, rights, keys, fresh):
        total = None if fresh else acc[...]
        for k in keys:
            term = dot(lefts[k], rights[k])
            total = term if total is None else total + term
        acc[...] = total

    def product_t(dzs, fresh=False, last=False):
        def product():
            gathered(acc_t, gb, qrb, [p.column(dz, dc) for dz in dzs for dc in (0, 1)], fresh)
            if last:
                t_own[...] = acc_t[...].astype(BF)
                tb[p.row()] = t_own[...]

        return product

    def rotate(keys, fresh=False):
        def rotated():
            gathered(rot, qlb, tb, [p.row(dy, dx) for dy, dx in keys], fresh)

        return rotated

    def moments():
        rotated = rot[...]
        first = decay_moment * mm[0].astype(F32) + (1.0 - decay_moment) * rotated
        second = decay_moment * mm[1].astype(F32) + (1.0 - decay_moment) * rotated * rotated
        direction = (first / (jnp.sqrt(second) + epsilon)).astype(BF)
        d_turned[...] = turned(direction).astype(BF)

    def left_term(k):
        return lax.dot_general(g[...], gcb[k], (((1,), (1,)), ((), ())), preferred_element_type=F32)

    def left_done(h, total):
        left[h] = total.astype(BF)

    def right_done(f, total):
        right_sum[half(f)] = total

    def right_term(k):
        return dot(g_turned[...], gb[k])

    backs = (back_0, back_1)

    def back_term(n):
        return lambda k: dot(d_turned[...], qlb[k, :, half(n)])

    def back_done(n):
        def store(f, total):
            backs[n][half(f)] = total.astype(BF)

        return store

    def update_term(n):
        return lambda k: dot(qrb[k], backs[n][...])

    def update_done(n):
        def store(rows, total):
            acc_t[rows, half(n)] = total

        return store

    def return_rotated():
        rot_0[...] = rot[...].astype(BF)
        move("rot", rot_0, rot_1)

    def return_right():
        right[...] = right_sum[...].T.astype(BF)
        move("right", right, right_1)

    def return_left():
        move("left", left, left_1)

    def return_update():
        u_0[...] = acc_t[...].T.astype(BF)
        move("u", u_0, u_1)

    def results():
        for name, src, dst in (("rot", rot_1, o_rot), ("right", right_1, o_r), ("left", left_1, o_l), ("u", u_1, o_u)):
            moved(name)
            dst[...] = src[...].astype(dst.dtype)

    near_rows = [(0, 0), (1, 0), (3, 0), (0, 1), (0, 3), (1, 1), (3, 1), (1, 3), (3, 3)]
    far_rows = [(2, 0), (0, 2), (2, 1), (2, 3), (1, 2), (3, 2), (2, 2)]
    gauge = {"gz": gb, "qp": qrb, "lz": qlb, "tp": tb, "b0": po_0, "b1": po_1, "u0": po_0, "u1": po_1, "gp": gcb, "ls": po_r, "rp": po_r}
    f = {name: w.flow(ref) for name, ref in gauge.items()}
    flows = {
        "mi": [move_in],
        "hg": [have_g],
        "hq": [have_qr],
        "hl": [have_ql],
        "mm": [move_moments],
        "hm": [have_moments],
        "gz": gather_z(f["gz"], p, g, gb),
        "qp": gather_plane(f["qp"], p, qr, qrb),
        "lz": gather_z(f["lz"], p, ql_turned, qlb),
        "t": [product_t([0, 1, 7, 2, 6], fresh=True), product_t([3, 5, 4], last=True)],
        "tp": gather_plane(f["tp"], p, t_own, tb),
        "r": [rotate(near_rows, fresh=True), rotate(far_rows), moments],
        "b0": scatter_plane(f["b0"], p, back_term(0), back_done(0), (pb_0, po_0, pi_0)),
        "b1": scatter_plane(f["b1"], p, back_term(1), back_done(1), (pb_1, po_1, pi_1)),
        "u0": scatter_z(f["u0"], p, update_term(0), update_done(0), (zb_0, zmo_0, zmi_0, zo_0, zi_0)),
        "u1": scatter_z(f["u1"], p, update_term(1), update_done(1), (zb_1, zmo_1, zmi_1, zo_1, zi_1)),
        "gp": gather_plane(f["gp"], p, g, gcb),
        "ls": scatter_z(f["ls"], p, left_term, left_done, (zb_l, zmo_l, zmi_l, zo_l, zi_l), parts=4),
        "rp": scatter_plane(f["rp"], p, right_term, right_done, (pb_r, po_r, pi_r)),
        "rr": [return_rotated],
        "rl": [return_left],
        "rt": [return_right],
        "ru": [return_update],
    }
    plan = [(t, step) for name, steps in flows.items() for t, step in zip(TIMES[name], steps, strict=True)]
    for _, step in sorted(plan, key=lambda item: item[0]):
        step()
    results()
    for flow in f.values():
        flow.drain()

    @pl.when(p.away)
    def _():
        for copy in moves.values():
            copy.wait_send()


def per_device(gradient, first_moment, second_moment, left_factor, right_factor, left_basis, right_basis):
    ins = [a.reshape(N, N) for a in (gradient, first_moment, second_moment, left_basis, right_basis)]
    block = pltpu.VMEM((N, N), BF)
    wide = pltpu.VMEM((N, N), F32)

    def many(n, dtype=BF, width=N):
        return pltpu.VMEM((n, N, width), dtype)

    rotated, left_sum, right_sum, update = pl.pallas_call(
        kernel,
        name="soap",
        out_shape=[jax.ShapeDtypeStruct((N, N), F32)] * 3 + [jax.ShapeDtypeStruct((N, N), BF)],
        in_specs=[pl.BlockSpec(memory_space=pl.ANY)] * 5,
        out_specs=[pl.BlockSpec(memory_space=pltpu.VMEM)] * 4,
        scratch_shapes=[block] * 3
        + [wide] * 2
        + [many(2)] * 2
        + [block] * 3
        + [many(16)] * 5
        + [block] * 12
        + [wide] * 3
        + [pltpu.VMEM((N, 128), BF)] * 2
        + ([many(16, F32, 128)] + [many(15, BF, 128)] * 2) * 2
        + [many(16, F32), many(15), many(15)]
        + ([many(8, F32, 128)] + [many(8, BF, 128)] * 2 + [many(7, BF, 128)] * 2) * 2
        + [many(8, F32), many(8), many(8), many(7), many(7)]
        + [pltpu.SemaphoreType.DMA((NSEND,)), pltpu.SemaphoreType.DMA((NRECV,))]
        + [pltpu.SemaphoreType.DMA((5,))],
        compiler_params=pltpu.CompilerParams(collective_id=0, has_side_effects=True, vmem_limit_bytes=60 * 1024 * 1024),
    )(*ins)
    rotated, left_sum, right_sum, update = (a.reshape(1, N, N) for a in (rotated, left_sum, right_sum, update))
    scale = 1.0 - decay_factor
    new_first = decay_moment * first_moment + (1.0 - decay_moment) * rotated
    new_second = decay_moment * second_moment + (1.0 - decay_moment) * rotated * rotated
    new_left = decay_factor * left_factor + scale * left_sum
    new_right = decay_factor * right_factor + scale * right_sum
    return (new_first, new_second, new_left, new_right, update)


def solution(mesh):
    spec = P(None, "mp", "dp")
    return jax.shard_map(
        per_device,
        mesh=mesh,
        in_specs=(spec,) * 5 + (P(None, "dp", "mp"), spec),
        out_specs=(spec,) * 5,
        check_vma=False,
    )
```

time: 456 us -> 103 us (0.23)
  waiting for transfers between devices: 245 us -> 0 us
  Pallas kernels: 0 us -> 97.6 us
  local copies, waits for them, and re-layouts: 92.9 us -> 0.68 us
  other arithmetic: 52.3 us -> 3.75 us
  starting transfers between devices: 30.7 us -> 0 us
  matrix products: 17.8 us -> 0 us
  between operations: 14.2 us -> 0.69 us
    all_gather x2 -> x0, waiting for transfers between devices: 167 us -> none  [the longest x1 99.2 us: turned_gather(): lax.all_gather(both, axis, axis=0, tiled=True)]
    pallas_call x0 -> x1, Pallas kernels: none -> 97.6 us  [per_device(): pl.pallas_call(kernel, name='soap', out_shape=[jax.ShapeDtypeStruct((N, N...]
    all_to_all x5 -> x0, waiting for transfers between devices: 78.4 us -> none  [the longest x1 41.9 us: per_device(): lax.all_to_all(column_grad, 'dp', split_axis=1, concat_axis=2, tiled=True)]
    unnamed x2 -> x0, other arithmetic: 44.5 us -> none
    all_to_all x5 -> x0, starting transfers between devices: 30.6 us -> none  [the longest x2 10.6 us: summed_on_arrival(): lax.all_to_all(pieces, axis, split_axis=0, concat_axis=0, tiled=True)]
    unnamed x23 -> x11, local copies, waits for them, and re-layouts: 31 us -> 0.68 us
    transpose x2 -> x0, local copies, waits for them, and re-layouts: 26.8 us -> none  [turned_gather(): gathered.append(jnp.moveaxis(section, 0, dim))]
    split x3 -> x0, local copies, waits for them, and re-layouts: 26.6 us -> none  [in_one_piece(): jnp.split(whole, [sum(widths[:k]) for k in range(1, len(widths))], axis=a...]
  transfers between devices with their start and end apart: 7 -> 0, of which waited for: 5 -> 0; matrix products, arithmetic and copies ran while one was open for 33% -> 0% of each run, Pallas kernels for 0% -> 0%
where the time goes in v2:
time: 103 us
  Pallas kernels  97.6 us (95%)
  other arithmetic  3.75 us (4%)
    pallas_call x1, Pallas kernels, per_device(): pl.pallas_call(kernel, name='soap', out_shape=[jax.ShapeDtypeStruct((N, N...  97.6 us

profile of v2, /device:TPU:1, one launch (start us, length us, event | category | flops | bytes accessed | tf_op | source)
XLA Modules:
  0.0 102.7 jit_solution(2230879270404966511)
XLA Ops:
  0.6 0.0 copy-start.2
  0.6 97.6 %soap.1 = (f32[256,256]{1,0:T(8,128)}, f32[256,256]{1,0:T(8,128)}, f32[256,256]{1,0:T(8,128)}, bf16[256,256]{1,0:T(8,128)(2,1)}) custom-call(bf16[256,256]{1,0:T(8,128)(2,1)} %bitcast.20, f32[256,256]{1,0:T(8,128)} %bitcast.18, f32[256,256]{1,0:T(8,128)} %bitcast.19, bf16[256,256]{1,0:T(8,128)(2,1)} %bitcast.21, bf16[256,256]{1,0:T(8,128)(2,1)} %bitcast.22), custom_call_target="tpu_custom_call" | custom-call | tf_op jit(solution)/shard_map/soap/pallas_call | solution.py:588
  98.2 0.0 copy-done.2
  98.3 0.0 copy-start
  98.3 0.0 copy-start.1
  98.3 0.0 copy-start.3
  98.3 1.8 %bitcast_add_fusion.1 = f32[1,256,256]{2,1,0:T(8,128)} fusion(f32[256,256]{1,0:T(8,128)} %get-tuple-element.10, f32[1,256,256]{2,1,0:T(8,128)S(1)} %copy-done.2), kind=kLoop, calls=%fused_computation.6 | loop fusion | flops 196608 | bytes 786432 | tf_op jit(solution)/shard_map/add | solution.py:614
  100.1 0.0 copy-done
  100.1 0.0 copy-done.1
  100.1 0.0 copy-done.3
  100.1 0.0 copy-start.4
  100.1 2.0 %fusion.2 = (f32[1,256,256]{2,1,0:T(8,128)}, f32[1,256,256]{2,1,0:T(8,128)}, f32[1,256,256]{2,1,0:T(8,128)}) fusion(f32[256,256]{1,0:T(8,128)} %get-tuple-element.9, f32[1,256,256]{2,1,0:T(8,128)S(1)} %copy-done.1, f32[1,256,256]{2,1,0:T(8,128)S(1)} %copy-done, f32[256,256]{1,0:T(8,128)} %get-tuple-element.11, f32[1,256,256]{2,1,0:T(8,128)S(1)} %copy-done.3), kind=kLoop, calls=%fused_computation.4 | loop fusion | flops 589824 | bytes 2097152 | tf_op jit(solution)/shard_map/add | solution.py:613
  102.1 0.0 copy-done.4
  102.1 0.7 copy.13
Async XLA Ops:
  0.6 97.6 %copy-start.2 = (f32[1,256,256]{2,1,0:T(8,128)S(1)}, f32[1,256,256]{2,1,0:T(8,128)}, u32[]{:S(2)}) copy-start(f32[1,256,256]{2,1,0:T(8,128)} %param.10) | copy-start | bytes 786436
  98.3 1.8 %copy-start = (f32[1,256,256]{2,1,0:T(8,128)S(1)}, f32[1,256,256]{2,1,0:T(8,128)}, u32[]{:S(2)}) copy-start(f32[1,256,256]{2,1,0:T(8,128)} %param.8) | copy-start | bytes 786436
  98.3 1.8 %copy-start.1 = (f32[1,256,256]{2,1,0:T(8,128)S(1)}, f32[1,256,256]{2,1,0:T(8,128)}, u32[]{:S(2)}) copy-start(f32[1,256,256]{2,1,0:T(8,128)} %param.9) | copy-start | bytes 786436
  98.3 1.8 %copy-start.3 = (f32[1,256,256]{2,1,0:T(8,128)S(1)}, f32[1,256,256]{2,1,0:T(8,128)}, u32[]{:S(2)}) copy-start(f32[1,256,256]{2,1,0:T(8,128)} %param.11) | copy-start | bytes 786436
  100.1 2.0 %copy-start.4 = (bf16[256,256]{1,0:T(8,128)(2,1)S(1)}, bf16[256,256]{1,0:T(8,128)(2,1)}, u32[]{:S(2)}) copy-start(bf16[256,256]{1,0:T(8,128)(2,1)} %get-tuple-element.12) | copy-start | bytes 393220

commit v3 on v2

--- a/solution.py
+++ b/solution.py
@@ -12,8 +12,9 @@
 NZ = 8
 NX = 4
 NY = 4
-NSEND = 19
-NRECV = 133
+NSEND = 22
+NRECV = 136
+LIMIT = 62
 
 BF = jnp.bfloat16
 F32 = jnp.float32
@@ -23,25 +24,25 @@
     "hg": (0.02,),
     "hq": (1.54,),
     "hl": (2.18,),
-    "mm": (34.45,),
-    "hm": (34.67,),
-    "gz": (2.12, 5.13, 5.87, 6.54, 7.24, 8.15, 8.88, 9.58, 10.29, 11.16, 11.89, 12.60, 13.30, 14.17, 14.90, 15.60, 16.31, 11.46, 17.45,),
-    "qp": (2.06, 5.79, 7.19, 8.81, 11.62, 13.73, 12.33, 17.95, 18.65,),
-    "lz": (16.00, 20.04, 20.08, 20.42, 21.12, 23.06, 23.79, 24.46, 25.17, 26.07, 26.80, 27.51, 28.21, 29.08, 29.81, 30.51, 31.22, 26.35, 32.30,),
-    "t": (18.67, 19.39,),
-    "tp": (19.98, 23.71, 25.12, 27.23, 30.04, 32.15, 30.74, 34.96, 35.66,),
-    "r": (32.32, 35.68, 36.32,),
-    "b0": (36.57, 37.12, 40.22, 40.92, 43.38, 41.33, 48.66, 51.74,),
-    "b1": (37.59, 38.14, 41.65, 42.33, 46.20, 42.68, 49.01, 52.72,),
-    "u0": (51.82, 52.16, 52.39, 53.70, 53.98, 54.44, 53.77, 53.82, 56.80, 56.86, 59.85, 60.55, 62.89, 63.59, 65.93, 66.64,),
-    "u1": (52.80, 53.14, 53.37, 54.94, 55.26, 55.75, 55.06, 55.00, 58.21, 58.27, 61.25, 61.96, 64.30, 65.00, 67.34, 68.04,),
-    "gp": (10.99, 15.92, 32.96, 22.38, 29.41, 33.63, 38.61, 33.55, 38.63,),
-    "ls": (38.65, 38.99, 39.22, 41.04, 41.60, 42.58, 41.11, 41.22, 41.16, 41.27, 44.15, 44.85, 44.21, 44.91, 47.19, 48.60, 47.89, 50.44, 50.50, 51.64, 50.94, 54.03, 54.19, 55.59, 54.89, 57.56,),
-    "rp": (49.27, 49.92, 53.88, 54.55, 57.66, 55.31, 63.99, 67.77,),
-    "rr": (46.61,),
-    "rl": (57.61,),
-    "rt": (67.85,),
-    "ru": (68.09,),
+    "mm": (12.00,),
+    "hm": (38.78,),
+    "gz": (2.12, 5.13, 5.87, 6.54, 7.24, 8.15, 8.88, 9.58, 10.29, 11.16, 11.89, 12.60, 13.30, 16.81, 17.51, 16.83, 17.54, 11.46, 18.68,),
+    "qp": (2.06, 5.79, 7.19, 10.73, 13.52, 15.63, 14.22, 19.83, 20.54,),
+    "lz": (10.66, 15.50, 16.21, 16.91, 17.61, 20.02, 21.28, 21.91, 22.12, 24.53, 25.79, 26.49, 27.20, 29.04, 30.30, 31.00, 31.71, 23.30, 32.79,),
+    "t": (20.56, 21.32,),
+    "tp": (21.95, 26.16, 27.57, 29.68, 32.49, 34.60, 33.45, 37.50, 38.12,),
+    "r": (32.81, 38.14, 38.80,),
+    "b0": (39.05, 39.60, 42.37, 43.98, 45.90, 44.10, 49.76, 53.30,),
+    "b1": (42.85, 43.40, 46.25, 46.95, 50.47, 47.30, 53.71, 56.79,),
+    "u0": (53.38, 53.81, 54.04, 55.17, 55.50, 55.99, 55.35, 55.30, 55.24, 55.41, 60.38, 60.44, 65.31, 66.02, 68.83, 69.53,),
+    "u1": (56.87, 57.21, 57.50, 58.67, 59.00, 59.49, 58.74, 58.85, 58.79, 58.91, 63.90, 64.61, 67.42, 68.13, 70.47, 71.17,),
+    "gp": (4.65, 18.70, 18.00, 25.03, 32.06, 35.58, 22.74, 37.52, 40.32,),
+    "ls": (40.34, 40.92, 41.58, 42.63, 43.87, 44.31, 42.75, 44.20, 44.26, 42.69, 43.92, 47.07, 46.35, 45.59, 48.69, 52.21, 51.51, 50.80, 53.24, 57.44, 58.09, 63.01, 57.91, 62.59, 63.30, 68.22,),
+    "rp": (36.33, 36.98, 41.41, 54.38, 51.14, 51.85, 61.11, 66.39,),
+    "rr": (57.83,),
+    "rl": (68.27,),
+    "rt": (66.47,),
+    "ru": (71.22,),
 }
 
 
@@ -341,14 +342,17 @@
         def step():
             if n < 3:
                 w.wait((n + 1, h), 8 // parts)
-            if n == 3:
+            if n == 2:
                 w.wait((4, h), 4 // parts)
             for way in WAYS if n < 4 else (last,):
                 total = base[(n * way) % 8, rows(h)]
-                if n < 3 or (n == 3 and way == last):
+                if n < 3:
                     total = total + into[slot(n + 1, way), rows(h)].astype(F32)
+                if n == 2 and way == last:
+                    total = total + into[0, rows(h)].astype(F32)
                 out[slot(n, way), rows(h)] = total.astype(BF)
-                w.send((n, h), out.at[slot(n, way), rows(h)], into.at[slot(n, way), rows(h)], p.device(dz=way))
+                to = p.device(dz=2 * way if n == 4 else way)
+                w.send((n, h), out.at[slot(n, way), rows(h)], into.at[slot(n, way), rows(h)], to)
 
         return step
 
@@ -384,6 +388,7 @@
     w = Wires(send_sem, recv_sem)
     home = jnp.logical_not(p.away)
     peers = [p.device(dz=1), p.device(dz=-1), p.device(dy=1), p.device(dy=-1), p.device(dx=1), p.device(dx=-1), p.device(dc=1), p.twin()]
+    peers += [p.device(dz=2), p.device(dz=-2), p.device(dx=2), p.device(dy=2)]
 
     barrier = pltpu.get_barrier_semaphore()
     for peer in peers:
@@ -395,7 +400,7 @@
         loads[name].start()
     loads["g"].wait()
     loads["qr"].wait()
-    pl.semaphore_wait(barrier, 8)
+    pl.semaphore_wait(barrier, len(peers))
 
     moves = {}
 
@@ -511,7 +516,8 @@
 
     def update_done(n):
         def store(rows, total):
-            acc_t[rows, half(n)] = total
+            u_0[half(n), rows] = total.T.astype(BF)
+            move(("u", n, rows.start), u_0.at[half(n), rows], u_1.at[half(n), rows])
 
         return store
 
@@ -526,14 +532,12 @@
     def return_left():
         move("left", left, left_1)
 
-    def return_update():
-        u_0[...] = acc_t[...].T.astype(BF)
-        move("u", u_0, u_1)
-
     def results():
-        for name, src, dst in (("rot", rot_1, o_rot), ("right", right_1, o_r), ("left", left_1, o_l), ("u", u_1, o_u)):
-            moved(name)
-            dst[...] = src[...].astype(dst.dtype)
+        for name in moves:
+            if name in ("rot", "right", "left") or name[0] == "u":
+                moved(name)
+        for src, dst in ((rot_1, o_rot), (right_1, o_r), (left_1, o_l), (u_1, o_u)):
+            dst[...] = src[...]
 
     near_rows = [(0, 0), (1, 0), (3, 0), (0, 1), (0, 3), (1, 1), (3, 1), (1, 3), (3, 3)]
     far_rows = [(2, 0), (0, 2), (2, 1), (2, 3), (1, 2), (3, 2), (2, 2)]
@@ -562,7 +566,6 @@
         "rr": [return_rotated],
         "rl": [return_left],
         "rt": [return_right],
-        "ru": [return_update],
     }
     plan = [(t, step) for name, steps in flows.items() for t, step in zip(TIMES[name], steps, strict=True)]
     for _, step in sorted(plan, key=lambda item: item[0]):
@@ -577,6 +580,16 @@
             copy.wait_send()
 
 
+def blend(rot, left, right, update, m1, m2, lf, rf, o_m1, o_m2, o_l, o_r, o_u):
+    rotated = rot[...].astype(F32)
+    scale = 1.0 - decay_factor
+    o_m1[...] = decay_moment * m1[...] + (1.0 - decay_moment) * rotated
+    o_m2[...] = decay_moment * m2[...] + (1.0 - decay_moment) * rotated * rotated
+    o_l[...] = decay_factor * lf[...] + scale * left[...].astype(F32)
+    o_r[...] = decay_factor * rf[...] + scale * right[...].astype(F32)
+    o_u[...] = update[...]
+
+
 def per_device(gradient, first_moment, second_moment, left_factor, right_factor, left_basis, right_basis):
     ins = [a.reshape(N, N) for a in (gradient, first_moment, second_moment, left_basis, right_basis)]
     block = pltpu.VMEM((N, N), BF)
@@ -585,11 +598,11 @@
     def many(n, dtype=BF, width=N):
         return pltpu.VMEM((n, N, width), dtype)
 
-    rotated, left_sum, right_sum, update = pl.pallas_call(
+    sums = pl.pallas_call(
         kernel,
         name="soap",
-        out_shape=[jax.ShapeDtypeStruct((N, N), F32)] * 3 + [jax.ShapeDtypeStruct((N, N), BF)],
-        in_specs=[pl.BlockSpec(memory_space=pl.ANY)] * 5,
+        out_shape=[jax.ShapeDtypeStruct((N, N), BF)] * 4,
+        in_specs=[pl.BlockSpec(memory_space=pltpu.HBM)] * 5,
         out_specs=[pl.BlockSpec(memory_space=pltpu.VMEM)] * 4,
         scratch_shapes=[block] * 3
         + [wide] * 2
@@ -605,15 +618,18 @@
         + [many(8, F32), many(8), many(8), many(7), many(7)]
         + [pltpu.SemaphoreType.DMA((NSEND,)), pltpu.SemaphoreType.DMA((NRECV,))]
         + [pltpu.SemaphoreType.DMA((5,))],
-        compiler_params=pltpu.CompilerParams(collective_id=0, has_side_effects=True, vmem_limit_bytes=60 * 1024 * 1024),
+        compiler_params=pltpu.CompilerParams(collective_id=0, has_side_effects=True, vmem_limit_bytes=LIMIT * 1024 * 1024),
     )(*ins)
-    rotated, left_sum, right_sum, update = (a.reshape(1, N, N) for a in (rotated, left_sum, right_sum, update))
-    scale = 1.0 - decay_factor
-    new_first = decay_moment * first_moment + (1.0 - decay_moment) * rotated
-    new_second = decay_moment * second_moment + (1.0 - decay_moment) * rotated * rotated
-    new_left = decay_factor * left_factor + scale * left_sum
-    new_right = decay_factor * right_factor + scale * right_sum
-    return (new_first, new_second, new_left, new_right, update)
+    old = [a.reshape(N, N) for a in (first_moment, second_moment, left_factor, right_factor)]
+    outs = pl.pallas_call(
+        blend,
+        name="blend",
+        out_shape=[jax.ShapeDtypeStruct((N, N), F32)] * 4 + [jax.ShapeDtypeStruct((N, N), BF)],
+        in_specs=[pl.BlockSpec(memory_space=pltpu.VMEM)] * 8,
+        out_specs=[pl.BlockSpec(memory_space=pltpu.VMEM)] * 5,
+        compiler_params=pltpu.CompilerParams(vmem_limit_bytes=LIMIT * 1024 * 1024),
+    )(*sums, *old)
+    return tuple(o.reshape(1, N, N) for o in outs)
 
 
 def solution(mesh):

time: 103 us -> 97.7 us (0.949)
  other arithmetic: 3.75 us -> 0 us
    add x2 -> x0, other arithmetic: 3.75 us -> none  [the longest x1 1.99 us: per_device(): decay_moment * second_moment + (1.0 - decay_moment) * rotated * rotated]
    pallas_call x1, Pallas kernels: 97.6 us -> 94.5 us  [per_device(): pl.pallas_call(kernel, name='soap', out_shape=[jax.ShapeDtypeStruct((N, N...]
    pallas_call x0 -> x1, Pallas kernels: none -> 2.53 us  [per_device(): pl.pallas_call(blend, name='blend', out_shape=[jax.ShapeDtypeStruct((N, N...]
where the time goes in v3:
time: 97.7 us; the launch traced here: 97.6 us
  Pallas kernels  97 us (99%)
    pallas_call x1, Pallas kernels, per_device(): pl.pallas_call(kernel, name='soap', out_shape=[jax.ShapeDtypeStruct((N, N...  94.5 us
    pallas_call x1, Pallas kernels, per_device(): pl.pallas_call(blend, name='blend', out_shape=[jax.ShapeDtypeStruct((N, N...  2.53 us

profile of v3, /device:TPU:1, one launch (start us, length us, event | category | flops | bytes accessed | tf_op | source)
XLA Modules:
  0.0 97.6 jit_solution(2586077594724396097)
XLA Ops:
  0.6 94.5 %soap.1 = (bf16[256,256]{1,0:T(8,128)(2,1)}, bf16[256,256]{1,0:T(8,128)(2,1)}, bf16[256,256]{1,0:T(8,128)(2,1)}, bf16[256,256]{1,0:T(8,128)(2,1)}) custom-call(bf16[256,256]{1,0:T(8,128)(2,1)} %bitcast.18, f32[256,256]{1,0:T(8,128)} %bitcast.12, f32[256,256]{1,0:T(8,128)} %bitcast.14, bf16[256,256]{1,0:T(8,128)(2,1)} %bitcast.19, bf16[256,256]{1,0:T(8,128)(2,1)} %bitcast.20), custom_call_target="tpu_custom_call" | custom-call | tf_op jit(solution)/shard_map/soap/pallas_call | solution.py:601
  95.1 2.5 %blend.1 = (f32[256,256]{1,0:T(8,128)}, f32[256,256]{1,0:T(8,128)}, f32[256,256]{1,0:T(8,128)}, f32[256,256]{1,0:T(8,128)}, bf16[256,256]{1,0:T(8,128)(2,1)}) custom-call(bf16[256,256]{1,0:T(8,128)(2,1)} %get-tuple-element.14.rot, bf16[256,256]{1,0:T(8,128)(2,1)} %get-tuple-element.15.left, bf16[256,256]{1,0:T(8,128)(2,1)} %get-tuple-element.16.right, ...), custom_call_target="tpu_custom_call" | custom-call | tf_op jit(solution)/shard_map/blend/pallas_call | solution.py:624

commit v4 on v3

--- a/solution.py
+++ b/solution.py
@@ -12,37 +12,35 @@
 NZ = 8
 NX = 4
 NY = 4
-NSEND = 22
-NRECV = 136
+NSEND = 25
+NRECV = 139
 LIMIT = 62
 
 BF = jnp.bfloat16
 F32 = jnp.float32
 MESH = pl.DeviceIdType.MESH
 TIMES = {
-    "mi": (0.00,),
-    "hg": (0.02,),
-    "hq": (1.54,),
-    "hl": (2.18,),
-    "mm": (12.00,),
-    "hm": (38.78,),
-    "gz": (2.12, 5.13, 5.87, 6.54, 7.24, 8.15, 8.88, 9.58, 10.29, 11.16, 11.89, 12.60, 13.30, 16.81, 17.51, 16.83, 17.54, 11.46, 18.68,),
-    "qp": (2.06, 5.79, 7.19, 10.73, 13.52, 15.63, 14.22, 19.83, 20.54,),
-    "lz": (10.66, 15.50, 16.21, 16.91, 17.61, 20.02, 21.28, 21.91, 22.12, 24.53, 25.79, 26.49, 27.20, 29.04, 30.30, 31.00, 31.71, 23.30, 32.79,),
-    "t": (20.56, 21.32,),
-    "tp": (21.95, 26.16, 27.57, 29.68, 32.49, 34.60, 33.45, 37.50, 38.12,),
-    "r": (32.81, 38.14, 38.80,),
-    "b0": (39.05, 39.60, 42.37, 43.98, 45.90, 44.10, 49.76, 53.30,),
-    "b1": (42.85, 43.40, 46.25, 46.95, 50.47, 47.30, 53.71, 56.79,),
-    "u0": (53.38, 53.81, 54.04, 55.17, 55.50, 55.99, 55.35, 55.30, 55.24, 55.41, 60.38, 60.44, 65.31, 66.02, 68.83, 69.53,),
-    "u1": (56.87, 57.21, 57.50, 58.67, 59.00, 59.49, 58.74, 58.85, 58.79, 58.91, 63.90, 64.61, 67.42, 68.13, 70.47, 71.17,),
-    "gp": (4.65, 18.70, 18.00, 25.03, 32.06, 35.58, 22.74, 37.52, 40.32,),
-    "ls": (40.34, 40.92, 41.58, 42.63, 43.87, 44.31, 42.75, 44.20, 44.26, 42.69, 43.92, 47.07, 46.35, 45.59, 48.69, 52.21, 51.51, 50.80, 53.24, 57.44, 58.09, 63.01, 57.91, 62.59, 63.30, 68.22,),
-    "rp": (36.33, 36.98, 41.41, 54.38, 51.14, 51.85, 61.11, 66.39,),
-    "rr": (57.83,),
-    "rl": (68.27,),
-    "rt": (66.47,),
-    "ru": (71.22,),
+    "mi": (0,),
+    "gz": (1, 2, 4, 6, 7, 10, 18, 11, 21, 17, 23, 19, 35, 29, 34, 31, 38, 41, 52, 39, 30, 53,),
+    "hq": (3,),
+    "qp": (5, 15, 24, 22, 28, 33, 45, 46, 48,),
+    "hl": (8,),
+    "gp": (9, 37, 47, 50, 67, 56, 63, 75, 65,),
+    "lz": (12, 13, 14, 16, 32, 25, 27, 26, 40, 43, 44, 36, 61, 60, 59, 51, 64, 70, 68, 66, 57, 72,),
+    "mm": (20,),
+    "hm": (42,),
+    "t": (49, 54,),
+    "tp": (55, 58, 73, 62, 69, 71, 82, 78, 80,),
+    "rp": (74, 111, 114, 121, 123, 129, 147, 159,),
+    "ls": (76, 79, 93, 81, 102, 113, 87, 91, 86, 88, 94, 100, 99, 95, 104, 106, 107, 110, 117, 122, 115, 120, 139, 155, 143, 144,),
+    "r": (77, 83, 84,),
+    "b0": (85, 90, 96, 97, 103, 101, 112, 118,),
+    "b1": (89, 92, 98, 105, 109, 108, 116, 128,),
+    "u0": (119, 124, 142, 125, 133, 146, 126, 127, 131, 132, 141, 145, 153, 156, 162, 163,),
+    "u1": (130, 134, 150, 135, 148, 154, 136, 138, 137, 140, 151, 152, 158, 160, 164, 165,),
+    "rr": (149,),
+    "rl": (157,),
+    "rt": (161,),
 }
 
 
@@ -146,12 +144,16 @@
     return {"dy": a, "dx": b} if f == 0 else {"dy": b, "dx": a}
 
 
-def gather_z(w, p, own, buf):
-    def start():
-        for h in range(4):
+def gather_z(w, p, own, buf, ready=lambda h: None):
+    def start(h):
+        def step():
+            ready(h)
             for way in WAYS:
                 w.send((1, h), own.at[part(h)], buf.at[p.column(), part(h)], p.device(dz=way))
-        w.send("C near", own, buf.at[p.column()], p.device(dc=1))
+            if h == 3:
+                w.send("C near", own, buf.at[p.column()], p.device(dc=1))
+
+        return step
 
     def arrive(n, h):
         last = WAYS[h // 2]
@@ -174,7 +176,7 @@
     def far_siblings():
         w.wait("C far", 4 * 3)
 
-    return [start] + [arrive(n, h) for n in (1, 2, 3, 4) for h in range(4)] + [near_siblings, far_siblings]
+    return [start(h) for h in range(4)] + [arrive(n, h) for n in (1, 2, 3, 4) for h in range(4)] + [near_siblings, far_siblings]
 
 
 def gather_plane(w, p, own, buf):
@@ -429,13 +431,11 @@
             moves[name].wait_recv()
 
     def move_in():
-        move("g", g_0, g)
+        for h in range(4):
+            move(("g", h), g_0.at[part(h)], g.at[part(h)])
         move("qr", qr_0, qr)
         loads["ql"].wait()
         move("ql", ql_0, ql)
-
-    def have_g():
-        moved("g")
 
     def have_qr():
         moved("qr")
@@ -545,12 +545,11 @@
     f = {name: w.flow(ref) for name, ref in gauge.items()}
     flows = {
         "mi": [move_in],
-        "hg": [have_g],
         "hq": [have_qr],
         "hl": [have_ql],
         "mm": [move_moments],
         "hm": [have_moments],
-        "gz": gather_z(f["gz"], p, g, gb),
+        "gz": gather_z(f["gz"], p, g, gb, lambda h: moved(("g", h))),
         "qp": gather_plane(f["qp"], p, qr, qrb),
         "lz": gather_z(f["lz"], p, ql_turned, qlb),
         "t": [product_t([0, 1, 7, 2, 6], fresh=True), product_t([3, 5, 4], last=True)],

time: 97.7 us -> 94.3 us (0.965)
  Pallas kernels: 97 us -> 93.6 us
    pallas_call x1, Pallas kernels: 94.5 us -> 91 us  [per_device(): pl.pallas_call(kernel, name='soap', out_shape=[jax.ShapeDtypeStruct((N, N...]
where the time goes in v4:
time: 94.3 us; the launch traced here: 94.2 us
  Pallas kernels  93.6 us (99%)
    pallas_call x1, Pallas kernels, per_device(): pl.pallas_call(kernel, name='soap', out_shape=[jax.ShapeDtypeStruct((N, N...  91 us
    pallas_call x1, Pallas kernels, per_device(): pl.pallas_call(blend, name='blend', out_shape=[jax.ShapeDtypeStruct((N, N...  2.53 us

profile of v4, /device:TPU:1, one launch (start us, length us, event | category | flops | bytes accessed | tf_op | source)
XLA Modules:
  0.0 94.2 jit_solution(9423935559461358067)
XLA Ops:
  0.6 91.0 %soap.1 = (bf16[256,256]{1,0:T(8,128)(2,1)}, bf16[256,256]{1,0:T(8,128)(2,1)}, bf16[256,256]{1,0:T(8,128)(2,1)}, bf16[256,256]{1,0:T(8,128)(2,1)}) custom-call(bf16[256,256]{1,0:T(8,128)(2,1)} %bitcast.18, f32[256,256]{1,0:T(8,128)} %bitcast.12, f32[256,256]{1,0:T(8,128)} %bitcast.14, bf16[256,256]{1,0:T(8,128)(2,1)} %bitcast.19, bf16[256,256]{1,0:T(8,128)(2,1)} %bitcast.20), custom_call_target="tpu_custom_call" | custom-call | tf_op jit(solution)/shard_map/soap/pallas_call | solution.py:600
  91.7 2.5 %blend.1 = (f32[256,256]{1,0:T(8,128)}, f32[256,256]{1,0:T(8,128)}, f32[256,256]{1,0:T(8,128)}, f32[256,256]{1,0:T(8,128)}, bf16[256,256]{1,0:T(8,128)(2,1)}) custom-call(bf16[256,256]{1,0:T(8,128)(2,1)} %get-tuple-element.14.rot, bf16[256,256]{1,0:T(8,128)(2,1)} %get-tuple-element.15.left, bf16[256,256]{1,0:T(8,128)(2,1)} %get-tuple-element.16.right, ...), custom_call_target="tpu_custom_call" | custom-call | tf_op jit(solution)/shard_map/blend/pallas_call | solution.py:623

commit v5 on v4

--- a/solution.py
+++ b/solution.py
@@ -76,6 +76,11 @@
         y = self.y + 1 - 2 * (self.y % 2)
         return {"dp": self.z * 2 + y % 2, "mp": (y // 2) * 8 + self.x * 2 + 1 - self.c}
 
+    def final(self, dz):
+        y = self.y + jnp.where(self.away, 1 - 2 * (self.y % 2), 0)
+        c = jnp.where(self.away, 1 - self.c, self.c)
+        return {"dp": lax.rem(self.z + dz + NZ, NZ) * 2 + y % 2, "mp": (y // 2) * 8 + self.x * 2 + c}
+
 
 class Wires:
     def __init__(self, send_sem, recv_sem):
@@ -308,7 +313,7 @@
     return [far, rest, near(2), near(1), opposite, near(0), beside, finish]
 
 
-def scatter_z(w, p, term, done, bufs, parts=2):
+def scatter_z(w, p, term, done, bufs, parts=2, move=None, moved=None):
     base, mate_out, mate_in, out, into = bufs
     stages = ((4, 3, 5), (2, 6), (1, 7, 0))
     size = N // parts
@@ -335,6 +340,10 @@
             w.wait(("C", k), 4 * len(stages[k]))
             for dz in stages[k]:
                 base[dz] = base[dz] + mate_in[dz].astype(F32)
+            if k == 2 and move:
+                out[7] = base[0].astype(BF)
+                for h in range(parts):
+                    move(h, out.at[7, rows(h)], into.at[7, rows(h)])
 
         return step
 
@@ -353,7 +362,7 @@
                 if n == 2 and way == last:
                     total = total + into[0, rows(h)].astype(F32)
                 out[slot(n, way), rows(h)] = total.astype(BF)
-                to = p.device(dz=2 * way if n == 4 else way)
+                to = p.final(way) if n == 1 and move else p.device(dz=2 * way if n == 4 else way)
                 w.send((n, h), out.at[slot(n, way), rows(h)], into.at[slot(n, way), rows(h)], to)
 
         return step
@@ -361,7 +370,11 @@
     def finish(h):
         def step():
             w.wait((1, h), 8 // parts)
-            total = base[0, rows(h)]
+            if move:
+                moved(h)
+                total = into[7, rows(h)].astype(F32)
+            else:
+                total = base[0, rows(h)]
             for way in WAYS:
                 total = total + into[slot(1, way), rows(h)].astype(F32)
             done(rows(h), total)
@@ -378,7 +391,7 @@
     g_0, ql_0, qr_0, m1_0, m2_0, mm_0, mm,
     g, ql, qr,
     gb, qlb, qrb, tb, gcb,
-    g_turned, ql_turned, t_own, d_turned, u_0, u_1,
+    g_turned, ql_turned, t_own, d_turned,
     left, left_1, right, right_1, rot_0, rot_1,
     acc_t, rot, right_sum,
     back_0, back_1,
@@ -390,7 +403,7 @@
     w = Wires(send_sem, recv_sem)
     home = jnp.logical_not(p.away)
     peers = [p.device(dz=1), p.device(dz=-1), p.device(dy=1), p.device(dy=-1), p.device(dx=1), p.device(dx=-1), p.device(dc=1), p.twin()]
-    peers += [p.device(dz=2), p.device(dz=-2), p.device(dx=2), p.device(dy=2)]
+    peers += [p.final(1), p.final(-1), p.device(dz=2), p.device(dz=-2), p.device(dx=2), p.device(dy=2)]
 
     barrier = pltpu.get_barrier_semaphore()
     for peer in peers:
@@ -516,10 +529,12 @@
 
     def update_done(n):
         def store(rows, total):
-            u_0[half(n), rows] = total.T.astype(BF)
-            move(("u", n, rows.start), u_0.at[half(n), rows], u_1.at[half(n), rows])
+            o_u[half(n), rows] = total.T.astype(BF)
 
         return store
+
+    def piece(n):
+        return lambda h, src, dst: move(("u", n, h), src, dst)
 
     def return_rotated():
         rot_0[...] = rot[...].astype(BF)
@@ -534,9 +549,9 @@
 
     def results():
         for name in moves:
-            if name in ("rot", "right", "left") or name[0] == "u":
+            if name in ("rot", "right", "left"):
                 moved(name)
-        for src, dst in ((rot_1, o_rot), (right_1, o_r), (left_1, o_l), (u_1, o_u)):
+        for src, dst in ((rot_1, o_rot), (right_1, o_r), (left_1, o_l)):
             dst[...] = src[...]
 
     near_rows = [(0, 0), (1, 0), (3, 0), (0, 1), (0, 3), (1, 1), (3, 1), (1, 3), (3, 3)]
@@ -557,8 +572,8 @@
         "r": [rotate(near_rows, fresh=True), rotate(far_rows), moments],
         "b0": scatter_plane(f["b0"], p, back_term(0), back_done(0), (pb_0, po_0, pi_0)),
         "b1": scatter_plane(f["b1"], p, back_term(1), back_done(1), (pb_1, po_1, pi_1)),
-        "u0": scatter_z(f["u0"], p, update_term(0), update_done(0), (zb_0, zmo_0, zmi_0, zo_0, zi_0)),
-        "u1": scatter_z(f["u1"], p, update_term(1), update_done(1), (zb_1, zmo_1, zmi_1, zo_1, zi_1)),
+        "u0": scatter_z(f["u0"], p, update_term(0), update_done(0), (zb_0, zmo_0, zmi_0, zo_0, zi_0), move=piece(0), moved=lambda h: moved(("u", 0, h))),
+        "u1": scatter_z(f["u1"], p, update_term(1), update_done(1), (zb_1, zmo_1, zmi_1, zo_1, zi_1), move=piece(1), moved=lambda h: moved(("u", 1, h))),
         "gp": gather_plane(f["gp"], p, g, gcb),
         "ls": scatter_z(f["ls"], p, left_term, left_done, (zb_l, zmo_l, zmi_l, zo_l, zi_l), parts=4),
         "rp": scatter_plane(f["rp"], p, right_term, right_done, (pb_r, po_r, pi_r)),
@@ -608,12 +623,12 @@
         + [many(2)] * 2
         + [block] * 3
         + [many(16)] * 5
-        + [block] * 12
+        + [block] * 10
         + [wide] * 3
         + [pltpu.VMEM((N, 128), BF)] * 2
         + ([many(16, F32, 128)] + [many(15, BF, 128)] * 2) * 2
         + [many(16, F32), many(15), many(15)]
-        + ([many(8, F32, 128)] + [many(8, BF, 128)] * 2 + [many(7, BF, 128)] * 2) * 2
+        + ([many(8, F32, 128)] + [many(8, BF, 128)] * 4) * 2
         + [many(8, F32), many(8), many(8), many(7), many(7)]
         + [pltpu.SemaphoreType.DMA((NSEND,)), pltpu.SemaphoreType.DMA((NRECV,))]
         + [pltpu.SemaphoreType.DMA((5,))],

time: 94.3 us -> 94.7 us (level)
  no operation moved by 1% of the time
where the time goes in v5:
time: 94.7 us; the launch traced here: 94.6 us
  Pallas kernels  94 us (99%)
    pallas_call x1, Pallas kernels, per_device(): pl.pallas_call(kernel, name='soap', out_shape=[jax.ShapeDtypeStruct((N, N...  91.4 us
    pallas_call x1, Pallas kernels, per_device(): pl.pallas_call(blend, name='blend', out_shape=[jax.ShapeDtypeStruct((N, N...  2.53 us

profile of v5, /device:TPU:1, one launch (start us, length us, event | category | flops | bytes accessed | tf_op | source)
XLA Modules:
  0.0 94.6 jit_solution(7400259838153740484)
XLA Ops:
  0.6 91.4 %soap.1 = (bf16[256,256]{1,0:T(8,128)(2,1)}, bf16[256,256]{1,0:T(8,128)(2,1)}, bf16[256,256]{1,0:T(8,128)(2,1)}, bf16[256,256]{1,0:T(8,128)(2,1)}) custom-call(bf16[256,256]{1,0:T(8,128)(2,1)} %bitcast.18, f32[256,256]{1,0:T(8,128)} %bitcast.12, f32[256,256]{1,0:T(8,128)} %bitcast.14, bf16[256,256]{1,0:T(8,128)(2,1)} %bitcast.19, bf16[256,256]{1,0:T(8,128)(2,1)} %bitcast.20), custom_call_target="tpu_custom_call" | custom-call | tf_op jit(solution)/shard_map/soap/pallas_call | solution.py:615
  92.1 2.5 %blend.1 = (f32[256,256]{1,0:T(8,128)}, f32[256,256]{1,0:T(8,128)}, f32[256,256]{1,0:T(8,128)}, f32[256,256]{1,0:T(8,128)}, bf16[256,256]{1,0:T(8,128)(2,1)}) custom-call(bf16[256,256]{1,0:T(8,128)(2,1)} %get-tuple-element.14.rot, bf16[256,256]{1,0:T(8,128)(2,1)} %get-tuple-element.15.left, bf16[256,256]{1,0:T(8,128)(2,1)} %get-tuple-element.16.right, ...), custom_call_target="tpu_custom_call" | custom-call | tf_op jit(solution)/shard_map/blend/pallas_call | solution.py:638
